TPU v7x, 8 devices: a whole 2x2x1 slice. The times are simulated.
8 devices in a mesh: stage: 1 (over z), data: 8 (over y, x, core).
Axes of the slice: x: 2, y: 2, z: 1, core: 2. Of those that a mesh axis runs over, the one named last changes fastest.
Arguments:
- w_master: float32 [32, 2048, 1408], P('stage', 'data')
- momentum: float32 [32, 2048, 1408], P('stage', 'data')
- grad: bfloat16 [32, 2048, 1408], P('stage', 'data')
Outputs:
- output 1: bfloat16 [32, 2048, 1408], P('stage')
- output 2: float32 [32, 2048, 1408], P('stage', 'data')
All inputs are finite; a program needn't handle non-finite values.
Results may differ from a plain program's by a relative error of at most 0.00743556.
Values are sent between devices in bfloat16 or wider.
A program may use at most 1.5 GiB of HBM per device.

v0:
```python
import math
import jax
import jax.numpy as jnp
from jax import lax
from jax.sharding import PartitionSpec as P

NS_ITERS = 5
MOMENTUM = 0.95
LEARN_RATE = 0.02
WEIGHT_DECAY = 0.1
NORM_EPS = 1e-7
COEF_A = 3.4445
COEF_B = -4.7750
COEF_C = 2.0315


def newton_schulz(x_mat):
    wide = x_mat.shape[1] <= x_mat.shape[2]
    for iteration in range(NS_ITERS):
        if wide:
            gram_mat = jnp.einsum("kip,kjp->kij", x_mat, x_mat, preferred_element_type=jnp.float32)
        else:
            gram_mat = jnp.einsum("kpi,kpj->kij", x_mat, x_mat, preferred_element_type=jnp.float32)
        gram_mat = gram_mat.astype(jnp.bfloat16)
        square = jnp.einsum("kij,kjl->kil", gram_mat, gram_mat, preferred_element_type=jnp.float32)
        poly_mat = (COEF_B * gram_mat.astype(jnp.float32) + COEF_C * square).astype(jnp.bfloat16)
        if wide:
            prod_mat = jnp.einsum("kij,kjp->kip", poly_mat, x_mat, preferred_element_type=jnp.float32)
        else:
            prod_mat = jnp.einsum("kpj,kij->kpi", x_mat, poly_mat, preferred_element_type=jnp.float32)
        x_mat = (COEF_A * x_mat.astype(jnp.float32) + prod_mat).astype(jnp.bfloat16)
    return x_mat


def solution(mesh):
    group = mesh.shape["data"]
    row_spec = P("stage", "data", None)
    full_spec = P("stage", None, None)

    def local_step(w_rows, mom_rows, grad_rows):
        mat_count, rows_dev, col_count = mom_rows.shape
        own_count = mat_count // group
        rms_scale = 0.2 * math.sqrt(max(rows_dev * group, col_count))
        mom_new = MOMENTUM * mom_rows + grad_rows.astype(jnp.float32)
        sq_total = lax.psum(jnp.sum(mom_new * mom_new, axis=(1, 2)), "data")
        owned = lax.all_to_all(mom_new.astype(jnp.bfloat16), "data", 0, 1, tiled=True)
        my_index = lax.axis_index("data")
        sq_owned = lax.dynamic_slice_in_dim(sq_total, my_index * own_count, own_count)
        x_mat = (owned.astype(jnp.float32) / (jnp.sqrt(sq_owned)[:, None, None] + NORM_EPS)).astype(jnp.bfloat16)
        x_mat = newton_schulz(x_mat)
        ortho_rows = lax.all_to_all(x_mat, "data", 1, 0, tiled=True)
        w_new = w_rows - LEARN_RATE * (ortho_rows.astype(jnp.float32) * rms_scale + WEIGHT_DECAY * w_rows)
        params = lax.all_gather(w_new.astype(jnp.bfloat16), "data", axis=1, tiled=True)
        return params, mom_new

    return jax.shard_map(local_step, mesh=mesh, in_specs=(row_spec, row_spec, row_spec), out_specs=(full_spec, row_spec), check_vma=False)
```

profile of v0, /device:TPU:0, one launch (start us, length us, event | category | flops | bytes accessed | tf_op | source)
XLA Modules:
  0.0 2373.3 jit_solution(1491309790090557894)
XLA Ops:
  7.2 38.9 %multiply_reduce_fusion = (f32[32]{0:T(128)S(1)}, f32[32,256,1408]{2,1,0:T(8,128)}) fusion(bf16[32,256,1408]{2,1,0:T(8,128)(2,1)} %param.5, f32[32,256,1408]{2,1,0:T(8,128)} %param.4), kind=kLoop, calls=%fused_computation.12 | loop fusion | flops 57671648 | bytes 115343488 | tf_op jit(solution)/shard_map/reduce_sum | solution.py:45
  76.0 269.1 %psum.7 = f32[32]{0:T(128)S(1)} all-reduce(f32[32]{0:T(128)S(1)} %get-tuple-element.2), channel_id=1, replica_groups=mesh['stage'=1,'data'=8] {'data'}, use_global_device_ids=true, to_apply=%region_1.0 | all-reduce | flops 32 | bytes 256 | tf_op jit(solution)/shard_map/psum | solution.py:45
  345.1 25.5 %copy.12 = f32[8,4,256,1408]{3,2,0,1:T(8,128)} copy(bf16[8,4,256,1408]{3,2,1,0:T(8,128)(2,1)} %bitcast.6) | data formatting | bytes 69206016 | tf_op jit(solution)/shard_map/convert_element_type | solution.py:49
  396.0 46.1 %convolution_convert_fusion.4 = bf16[4,1408,1408]{2,1,0:T(8,128)(2,1)} fusion(bf16[4,2048,1408]{2,1,0:T(8,128)(2,1)} %fusion), kind=kOutput, calls=%fused_computation.33 | convolution fusion | flops 32488620032 | bytes 38928384 | tf_op jit(solution)/shard_map/kpi,kpj->kij/dot_general | solution.py:23
  442.1 37.3 %fusion.13 = bf16[4,1408,1408]{2,1,0:T(8,128)(2,1)} fusion(bf16[4,1408,1408]{2,1,0:T(8,128)(2,1)} %convolution_convert_fusion.4), kind=kOutput, calls=%fused_computation.28 | convolution fusion | flops 22370123776 | bytes 31719424 | tf_op jit(solution)/shard_map/kij,kjl->kil/dot_general | solution.py:25
  479.4 50.1 %add_convert_fusion.4 = bf16[4,2048,1408]{2,1,0:T(8,128)(2,1)} fusion(bf16[4,2048,1408]{2,1,0:T(8,128)(2,1)} %fusion, bf16[4,1408,1408]{2,1,0:T(8,128)(2,1)} %fusion.13), kind=kOutput, calls=%fused_computation.11 | convolution fusion | flops 32526827520 | bytes 61997056 | tf_op jit(solution)/shard_map/kpj,kij->kpi/dot_general | solution.py:30
  529.5 46.3 %convolution_convert_fusion.3 = bf16[4,1408,1408]{2,1,0:T(8,128)(2,1)} fusion(bf16[4,2048,1408]{2,1,0:T(8,128)(2,1)} %add_convert_fusion.4), kind=kOutput, calls=%fused_computation.32 | convolution fusion | flops 32488620032 | bytes 38928384 | tf_op jit(solution)/shard_map/kpi,kpj->kij/dot_general | solution.py:23
  575.8 37.6 %fusion.12 = bf16[4,1408,1408]{2,1,0:T(8,128)(2,1)} fusion(bf16[4,1408,1408]{2,1,0:T(8,128)(2,1)} %convolution_convert_fusion.3), kind=kOutput, calls=%fused_computation.27 | convolution fusion | flops 22370123776 | bytes 31719424 | tf_op jit(solution)/shard_map/kij,kjl->kil/dot_general | solution.py:25
  613.4 50.0 %add_convert_fusion.3 = bf16[4,2048,1408]{2,1,0:T(8,128)(2,1)} fusion(bf16[4,2048,1408]{2,1,0:T(8,128)(2,1)} %add_convert_fusion.4, bf16[4,1408,1408]{2,1,0:T(8,128)(2,1)} %fusion.12), kind=kOutput, calls=%fused_computation.10 | convolution fusion | flops 32526827520 | bytes 61997056 | tf_op jit(solution)/shard_map/kpj,kij->kpi/dot_general | solution.py:30
  663.5 46.2 %convolution_convert_fusion.2 = bf16[4,1408,1408]{2,1,0:T(8,128)(2,1)} fusion(bf16[4,2048,1408]{2,1,0:T(8,128)(2,1)} %add_convert_fusion.3), kind=kOutput, calls=%fused_computation.31 | convolution fusion | flops 32488620032 | bytes 38928384 | tf_op jit(solution)/shard_map/kpi,kpj->kij/dot_general | solution.py:23
  709.7 37.4 %fusion.11 = bf16[4,1408,1408]{2,1,0:T(8,128)(2,1)} fusion(bf16[4,1408,1408]{2,1,0:T(8,128)(2,1)} %convolution_convert_fusion.2), kind=kOutput, calls=%fused_computation.26 | convolution fusion | flops 22370123776 | bytes 31719424 | tf_op jit(solution)/shard_map/kij,kjl->kil/dot_general | solution.py:25
  747.1 50.1 %add_convert_fusion.2 = bf16[4,2048,1408]{2,1,0:T(8,128)(2,1)} fusion(bf16[4,2048,1408]{2,1,0:T(8,128)(2,1)} %add_convert_fusion.3, bf16[4,1408,1408]{2,1,0:T(8,128)(2,1)} %fusion.11), kind=kOutput, calls=%fused_computation.9 | convolution fusion | flops 32526827520 | bytes 61997056 | tf_op jit(solution)/shard_map/kpj,kij->kpi/dot_general | solution.py:30
  797.2 46.5 %convolution_convert_fusion.1 = bf16[4,1408,1408]{2,1,0:T(8,128)(2,1)} fusion(bf16[4,2048,1408]{2,1,0:T(8,128)(2,1)} %add_convert_fusion.2), kind=kOutput, calls=%fused_computation.30 | convolution fusion | flops 32488620032 | bytes 38928384 | tf_op jit(solution)/shard_map/kpi,kpj->kij/dot_general | solution.py:23
  843.7 37.3 %fusion.10 = bf16[4,1408,1408]{2,1,0:T(8,128)(2,1)} fusion(bf16[4,1408,1408]{2,1,0:T(8,128)(2,1)} %convolution_convert_fusion.1), kind=kOutput, calls=%fused_computation.25 | convolution fusion | flops 22370123776 | bytes 31719424 | tf_op jit(solution)/shard_map/kij,kjl->kil/dot_general | solution.py:25
  881.0 50.0 %add_convert_fusion.1 = bf16[4,2048,1408]{2,1,0:T(8,128)(2,1)} fusion(bf16[4,2048,1408]{2,1,0:T(8,128)(2,1)} %add_convert_fusion.2, bf16[4,1408,1408]{2,1,0:T(8,128)(2,1)} %fusion.10), kind=kOutput, calls=%fused_computation.8 | convolution fusion | flops 32526827520 | bytes 61997056 | tf_op jit(solution)/shard_map/kpj,kij->kpi/dot_general | solution.py:30
  931.1 46.3 %convolution_convert_fusion = bf16[4,1408,1408]{2,1,0:T(8,128)(2,1)} fusion(bf16[4,2048,1408]{2,1,0:T(8,128)(2,1)} %add_convert_fusion.1), kind=kOutput, calls=%fused_computation.29 | convolution fusion | flops 32488620032 | bytes 38928384 | tf_op jit(solution)/shard_map/kpi,kpj->kij/dot_general | solution.py:23
  977.3 37.4 %fusion.9 = bf16[4,1408,1408]{2,1,0:T(8,128)(2,1)} fusion(bf16[4,1408,1408]{2,1,0:T(8,128)(2,1)} %convolution_convert_fusion), kind=kOutput, calls=%fused_computation.24 | convolution fusion | flops 22370123776 | bytes 31719424 | tf_op jit(solution)/shard_map/kij,kjl->kil/dot_general | solution.py:25
  1014.8 50.1 %add_convert_fusion = bf16[4,2048,1408]{2,1,0:T(8,128)(2,1)} fusion(bf16[4,2048,1408]{2,1,0:T(8,128)(2,1)} %add_convert_fusion.1, bf16[4,1408,1408]{2,1,0:T(8,128)(2,1)} %fusion.9), kind=kOutput, calls=%fused_computation.7 | convolution fusion | flops 32526827520 | bytes 61997056 | tf_op jit(solution)/shard_map/kpj,kij->kpi/dot_general | solution.py:30
  1064.8 29.8 %copy.18 = bf16[4,2048,1408]{2,0,1:T(4,128)(2,1)} copy(bf16[4,2048,1408]{2,1,0:T(8,128)(2,1)} %add_convert_fusion) | data formatting | bytes 46137344 | tf_op jit(solution)/shard_map/convert_element_type | solution.py:31
  1094.6 259.1 %all_to_all.8 = bf16[4,2048,1408]{2,0,1:T(4,128)(2,1)} all-to-all(bf16[4,2048,1408]{2,0,1:T(4,128)(2,1)} %copy.18), channel_id=1, replica_groups=mesh['stage'=1,'data'=8] {'data'}, dimensions={1} | all-to-all | bytes 46137344 | tf_op jit(solution)/shard_map/all_to_all | solution.py:51
  1376.3 36.5 %copy.19 = f32[8,4,256,1408]{3,2,1,0:T(8,128)} copy(f32[8,4,256,1408]{3,1,2,0:T(4,128)} %bitcast.49) | data formatting | bytes 92274688 | tf_op jit(solution)/shard_map/mul | solution.py:52
  1412.8 37.6 %fusion.3 = bf16[32,256,1408]{2,1,0:T(8,128)(2,1)} fusion(f32[32,256,1408]{2,1,0:T(8,128)} %param.3, f32[8,4,256,1408]{3,2,1,0:T(8,128)} %copy.19), kind=kLoop, calls=%fused_computation.5 | loop fusion | flops 57671680 | bytes 115343360 | tf_op jit(solution)/shard_map/convert_element_type | solution.py:53
  1450.4 794.5 %all-gather.2.cloned.1.call-done = bf16[32,2048,1408]{2,1,0:T(8,128)(2,1)} async-done(((bf16[32,256,1408]{2,1,0:T(8,128)(2,1)}), bf16[32,2048,1408]{2,1,0:T(8,128)(2,1)}) %all-gather.2.cloned.1.call-update) | async-done | bytes 184549392 | tf_op jit(solution)/shard_map/all_gather | solution.py:53
  2244.9 121.1 %copy.26 = bf16[32,2048,1408]{2,1,0:T(8,128)(2,1)} copy(bf16[32,2048,1408]{2,1,0:T(8,128)(2,1)} %all-gather.2.cloned.1.call-done) | data formatting | bytes 369098752
  (8 shorter events, 78.0 us)
Async XLA Ops:
  70.9 274.2 %all-to-all-start = ((bf16[32,256,1408]{2,1,0:T(8,128)(2,1)}), bf16[32,256,1408]{2,1,0:T(8,128)(2,1)}, u32[]{:S(2)}, u32[]{:S(2)}) async-start(bf16[32,256,1408]{2,1,0:T(8,128)(2,1)} %convert_element_type.106), calls=%async_computation | async-start | bytes 46137344 | tf_op jit(solution)/shard_map/all_to_all | solution.py:46
  75.9 2169.0 %all-gather.2.cloned.1.call-start = ((), (), s32[]{:S(2)}) async-start(), calls=%async_computation.2 | async-start | bytes 207618048 | tf_op jit(solution)/shard_map/all_gather | solution.py:53
Sparse Core Ops, SparseCore 0:
  1450.5 794.2 all-gather.1
where the time goes:
time: 2380 us; the launch traced here: 2370 us
  waiting for transfers between devices  794 us (33%)
  matrix products  669 us (28%)
  blocking collectives  528 us (22%)
  local copies, waits for them, and re-layouts  213 us (9%)
  other arithmetic  149 us (6%)
    all_gather x1, waiting for transfers between devices, local_step(): lax.all_gather(w_new.astype(jnp.bfloat16), 'data', axis=1, tiled=True)  794 us
    psum x1, blocking collectives, local_step(): sq_total = lax.psum(jnp.sum(mom_new * mom_new, axis=(1, 2)), 'data')  269 us
    all_to_all x1, blocking collectives, local_step(): ortho_rows = lax.all_to_all(x_mat, 'data', 1, 0, tiled=True)  259 us
    dot_general x5, matrix products, newton_schulz(): jnp.einsum('kpj,kij->kpi', x_mat, poly_mat, preferred_element_type=jnp.fl...  250 us
    dot_general x5, matrix products, newton_schulz(): jnp.einsum('kpi,kpj->kij', x_mat, x_mat, preferred_element_type=jnp.float32)  231 us
    dot_general x5, matrix products, newton_schulz(): jnp.einsum('kij,kjl->kil', gram_mat, gram_mat, preferred_element_type=jnp...  187 us
    unnamed x1, local copies, waits for them, and re-layouts  121 us
  transfers between devices with their start and end apart: 2, of which 1 were waited for; matrix products, arithmetic and copies ran while one was open for 0% of the time, Pallas kernels for 0%

commit v1 on v0

v1 whole, which is shorter than its diff:
```python
import math
import jax
import jax.numpy as jnp
from jax import lax
from jax.experimental import pallas as pl
from jax.sharding import PartitionSpec as P

NS_ITERS = 5
MOMENTUM = 0.95
LEARN_RATE = 0.02
WEIGHT_DECAY = 0.1
NORM_EPS = 1e-7
COEF_A = 3.4445
COEF_B = -4.7750
COEF_C = 2.0315
COPY_ROWS = 1024
LAST_SPLIT = 6


def after(value, *deps):
    return lax.optimization_barrier((value, *deps))[0]


def ns_step(x_mat):
    wide = x_mat.shape[0] <= x_mat.shape[1]
    eq = "ip,jp->ij" if wide else "pi,pj->ij"
    gram_mat = jnp.einsum(eq, x_mat, x_mat, preferred_element_type=jnp.float32).astype(jnp.bfloat16)
    square = jnp.dot(gram_mat, gram_mat, preferred_element_type=jnp.float32)
    poly_mat = (COEF_B * gram_mat.astype(jnp.float32) + COEF_C * square).astype(jnp.bfloat16)
    poly_mat = lax.optimization_barrier(poly_mat)
    eq = "ij,jp->ip" if wide else "ij,pj->pi"
    prod_mat = jnp.einsum(eq, poly_mat, x_mat, preferred_element_type=jnp.float32)
    return (COEF_A * x_mat.astype(jnp.float32) + prod_mat).astype(jnp.bfloat16)


def momentum_body(*refs):
    mom_ref, grad_ref = refs[:2]
    new_ref, low_ref, sum_ref = refs[-3:]
    new = MOMENTUM * mom_ref[...] + grad_ref[...].astype(jnp.float32)
    new_ref[...] = new
    low_ref[...] = new.astype(jnp.bfloat16)
    sum_ref[...] = jnp.broadcast_to(jnp.sum(new * new), sum_ref.shape)


def momentum_rows(mom_rows, grad_rows, whole, first, waves, group):
    total, rows, cols = mom_rows.shape
    here = pl.BlockSpec((1, rows, cols), lambda k, d: (first + k * group + d, 0, 0))
    in_specs, operands, aliases = [here, here], [mom_rows, grad_rows], {}
    if whole is not None:
        in_specs.append(pl.BlockSpec(memory_space=pl.ANY))
        operands.append(whole)
        aliases = {2: 0}
    count = waves * group
    return pl.pallas_call(
        momentum_body,
        grid=(waves, group),
        in_specs=in_specs,
        out_specs=(
            here,
            pl.BlockSpec((1, rows, cols), lambda k, d: (d * waves + k, 0, 0)),
            pl.BlockSpec((1, 8, 128), lambda k, d: (d * waves + k, 0, 0)),
        ),
        out_shape=(
            jax.ShapeDtypeStruct((total, rows, cols), jnp.float32),
            jax.ShapeDtypeStruct((count, rows, cols), jnp.bfloat16),
            jax.ShapeDtypeStruct((count, 8, 128), jnp.float32),
        ),
        input_output_aliases=aliases,
        cost_estimate=pl.CostEstimate(flops=4 * count * rows * cols, bytes_accessed=12 * count * rows * cols, transcendentals=0),
    )(*operands)


def place_body(*refs):
    refs[-1][...] = refs[0][...]


def place(whole, piece, first, total):
    mats, rows, cols = piece.shape
    step = math.gcd(rows, COPY_ROWS)
    in_specs = [pl.BlockSpec((1, step, cols), lambda i, j: (i, j, 0))]
    operands = [piece]
    aliases = {}
    if whole is not None:
        in_specs.append(pl.BlockSpec(memory_space=pl.ANY))
        operands.append(whole)
        aliases = {1: 0}
    return pl.pallas_call(
        place_body,
        grid=(mats, rows // step),
        in_specs=in_specs,
        out_specs=pl.BlockSpec((1, step, cols), lambda i, j: (i + first, j, 0)),
        out_shape=jax.ShapeDtypeStruct((total, rows, cols), piece.dtype),
        input_output_aliases=aliases,
        cost_estimate=pl.CostEstimate(flops=2 * piece.size, bytes_accessed=4 * piece.size, transcendentals=0),
    )(*operands)


def solution(mesh):
    group = mesh.shape["data"]
    row_spec = P("stage", "data", None)
    full_spec = P("stage", None, None)

    def local_step(w_rows, mom_rows, grad_rows):
        mat_count, rows_dev, col_count = mom_rows.shape
        waves = mat_count // group
        rest = waves - 1
        rows_all = rows_dev * group
        rms_scale = 0.2 * math.sqrt(max(rows_all, col_count))

        def exchange(array):
            return lax.all_to_all(array, "data", 0, 0, tiled=True)

        mom_new, low_0, sum_0 = momentum_rows(mom_rows, grad_rows, None, 0, 1, group)
        mom_new, low_r, sum_r = momentum_rows(mom_rows, grad_rows, mom_new, group, rest, group)
        sum_0 = exchange(sum_0)
        low_0 = exchange(after(low_0, sum_0))
        sum_r = exchange(after(sum_r, low_0))
        low_r = exchange(after(low_r, sum_r)).reshape(group, rest, rows_dev, col_count)
        sum_r = sum_r.reshape(group, rest, 8, 128)

        def begin(wave):
            low, part = (low_0, sum_0[:, 0, 0]) if wave == 0 else (low_r[:, wave - 1], sum_r[:, wave - 1, 0, 0])
            whole = low.reshape(rows_all, col_count).astype(jnp.float32)
            return (whole / (jnp.sqrt(jnp.sum(part)) + NORM_EPS)).astype(jnp.bfloat16)

        def finish(x_mat, wave):
            ortho = exchange(x_mat.reshape(group, rows_dev, col_count))
            w_old = lax.slice_in_dim(w_rows, wave * group, (wave + 1) * group)
            w_new = w_old - LEARN_RATE * (ortho.astype(jnp.float32) * rms_scale + WEIGHT_DECAY * w_old)
            return lax.optimization_barrier(w_new.astype(jnp.bfloat16))

        updates = {(1, 2): 0, (2, 4): 1, (3, 4): 2}
        rows_low = [None] * waves
        pieces = []
        x_mat = None
        for wave in range(waves):
            x_mat = begin(wave) if x_mat is None else after(begin(wave), x_mat)
            for iteration in range(NS_ITERS):
                if (wave, iteration) in updates:
                    x_mat = after(x_mat, rows_low[updates[wave, iteration]])
                x_mat = ns_step(x_mat)
                x_mat = lax.optimization_barrier(x_mat)
            rows_low[wave] = finish(x_mat, wave)
            cuts = (0, LAST_SPLIT, group) if wave == waves - 1 else (0, group)
            for low, high in zip(cuts, cuts[1:]):
                part = lax.slice_in_dim(rows_low[wave], low, high)
                pieces.append((wave * group + low, lax.all_gather(part, "data", axis=1, tiled=True)))
        params = None
        for first, piece in pieces:
            params = place(params, after(piece, x_mat), first, mat_count)
        return params, mom_new

    return jax.shard_map(local_step, mesh=mesh, in_specs=(row_spec, row_spec, row_spec), out_specs=(full_spec, row_spec), check_vma=False)
```

time: 2380 us -> 2080 us (0.87)
  blocking collectives: 528 us -> 77.1 us
  waiting for transfers between devices: 794 us -> 1110 us
  local copies, waits for them, and re-layouts: 213 us -> 7.41 us
  Pallas kernels: 0 us -> 197 us
  matrix products: 669 us -> 577 us
  other arithmetic: 149 us -> 61.4 us
    all_to_all x1 -> x6, waiting for transfers between devices: 0.01 us -> 331 us  [exchange(): return lax.all_to_all(array, 'data', 0, 0, tiled=True)]
    psum x1 -> x0, blocking collectives: 269 us -> none  [local_step(): sq_total = lax.psum(jnp.sum(mom_new * mom_new, axis=(1, 2)), 'data')]
    pallas_call x0 -> x7, Pallas kernels: none -> 197 us  [the longest x5 140 us: place(): pl.pallas_call(place_body, grid=(mats, rows // step), in_specs=in_specs,...]
    all_to_all x1 -> x2, blocking collectives: 259 us -> 77.1 us  [exchange(): return lax.all_to_all(array, 'data', 0, 0, tiled=True)]
    unnamed x1 -> x26, local copies, waits for them, and re-layouts: 121 us -> 0.07 us
    dot_general x15 -> x60, matrix products: 669 us -> 577 us  [the longest x20 223 us: ns_step(): jnp.einsum(eq, poly_mat, x_mat, preferred_element_type=jnp.float32)]
    convert_element_type x2 -> x0, local copies, waits for them, and re-layouts: 55.3 us -> none  [the longest x1 29.8 us: newton_schulz(): x_mat = (COEF_A * x_mat.astype(jnp.float32) + prod_mat).astype(jnp.bfloat16)]
    reduce_sum x1 -> x2, other arithmetic: 38.9 us -> 1.35 us  [begin(): return (whole / (jnp.sqrt(jnp.sum(part)) + NORM_EPS)).astype(jnp.bfloat16)]
  transfers between devices with their start and end apart: 2 -> 11, of which waited for: 1 -> 10; matrix products, arithmetic and copies ran while one was open for 0% -> 5% of each run, Pallas kernels for 0% -> 5%
where the time goes in v1:
time: 2080 us; the launch traced here: 2070 us
  waiting for transfers between devices  1110 us (53%)
  matrix products  577 us (28%)
  Pallas kernels  197 us (9%)
  blocking collectives  77.1 us (4%)
  other arithmetic  61.4 us (3%)
  starting transfers between devices  21 us (1%)
    all_gather x5, waiting for transfers between devices, local_step(): lax.all_gather(part, 'data', axis=1, tiled=True)  777 us
    all_to_all x6, waiting for transfers between devices, exchange(): return lax.all_to_all(array, 'data', 0, 0, tiled=True)  331 us
    dot_general x20, matrix products, ns_step(): jnp.einsum(eq, poly_mat, x_mat, preferred_element_type=jnp.float32)  223 us
    dot_general x20, matrix products, ns_step(): jnp.einsum(eq, x_mat, x_mat, preferred_element_type=jnp.float32)  211 us
    dot_general x20, matrix products, ns_step(): square = jnp.dot(gram_mat, gram_mat, preferred_element_type=jnp.float32)  143 us
    pallas_call x5, Pallas kernels, place(): pl.pallas_call(place_body, grid=(mats, rows // step), in_specs=in_specs,...  140 us
    all_to_all x2, blocking collectives, exchange(): return lax.all_to_all(array, 'data', 0, 0, tiled=True)  77.1 us
    pallas_call x2, Pallas kernels, momentum_rows(): pl.pallas_call(momentum_body, grid=(waves, group), in_specs=in_specs, out...  56.9 us
  transfers between devices with their start and end apart: 11, of which 10 were waited for; matrix products, arithmetic and copies ran while one was open for 5% of the time, Pallas kernels for 5%

profile of v1, /device:TPU:0, one launch (start us, length us, event | category | flops | bytes accessed | tf_op | source)
XLA Modules:
  0.0 2067.7 jit_solution(995564309602265226)
XLA Ops:
  7.2 14.6 shard_map.50
  34.3 42.3 %shard_map.51 = (f32[32,256,1408]{2,1,0:T(8,128)}, bf16[24,256,1408]{2,1,0:T(8,128)(2,1)}, f32[24,8,128]{2,1,0:T(8,128)}) custom-call(f32[32,256,1408]{2,1,0:T(8,128)} %refs_0_.3, bf16[32,256,1408]{2,1,0:T(8,128)(2,1)} %refs_1_.3, f32[32,256,1408]{2,1,0:T(8,128)} %get-tuple-element.22.refs_2_), custom_call_target="tpu_custom_call", output_to_operand_aliasing={{0}: (2, {})} | custom-call | flops 34603008 | bytes 103809024 | tf_op jit(solution)/shard_map/pallas_call | solution.py:54
  77.9 22.3 %all-to-all-done.1 = bf16[8,256,1408]{2,1,0:T(8,128)(2,1)} async-done(((bf16[8,256,1408]{2,1,0:T(8,128)(2,1)}), bf16[8,256,1408]{2,1,0:T(8,128)(2,1)}, u32[]{:S(2)}, u32[]{:S(2)}) %all-to-all-start.1) | async-done | bytes 5767200 | tf_op jit(solution)/shard_map/all_to_all | solution.py:111
  232.4 15.9 add_convert_fusion.15
  251.8 66.0 %all-to-all-done.4 = bf16[8,256,1408]{2,1,0:T(8,128)(2,1)} async-done(((bf16[8,256,1408]{2,1,0:T(8,128)(2,1)}), bf16[8,256,1408]{2,1,0:T(8,128)(2,1)}, u32[]{:S(2)}, u32[]{:S(2)}) %all-to-all-start.4) | async-done | bytes 5767200 | tf_op jit(solution)/shard_map/all_to_all | solution.py:111
  336.3 175.9 %all-to-all-done.3 = bf16[24,256,1408]{2,1,0:T(8,128)(2,1)} async-done(((bf16[24,256,1408]{2,1,0:T(8,128)(2,1)}), bf16[24,256,1408]{2,1,0:T(8,128)(2,1)}, u32[]{:S(2)}, u32[]{:S(2)}) %all-to-all-start.3) | async-done | bytes 17301536 | tf_op jit(solution)/shard_map/all_to_all | solution.py:111
  512.2 12.3 divide_convert_fusion.1
  650.8 14.2 add_convert_fusion.10
  751.5 13.2 convolution_convert_fusion.6
  783.9 33.5 %all-to-all-done.5 = bf16[8,256,1408]{2,1,0:T(8,128)(2,1)} async-done(((bf16[8,256,1408]{2,1,0:T(8,128)(2,1)}), bf16[8,256,1408]{2,1,0:T(8,128)(2,1)}, u32[]{:S(2)}, u32[]{:S(2)}) %all-to-all-start.5) | async-done | bytes 5767200 | tf_op jit(solution)/shard_map/all_to_all | solution.py:111
  828.4 13.7 convolution_convert_fusion.5
  947.6 13.2 convolution_convert_fusion.1
  979.9 33.6 %all-to-all-done.6 = bf16[8,256,1408]{2,1,0:T(8,128)(2,1)} async-done(((bf16[8,256,1408]{2,1,0:T(8,128)(2,1)}), bf16[8,256,1408]{2,1,0:T(8,128)(2,1)}, u32[]{:S(2)}, u32[]{:S(2)}) %all-to-all-start.6) | async-done | bytes 5767200 | tf_op jit(solution)/shard_map/all_to_all | solution.py:111
  1024.5 13.7 convolution_convert_fusion
  1055.6 68.0 %all_to_all.41 = bf16[8,256,1408]{2,1,0:T(8,128)(2,1)} all-to-all(bf16[8,256,1408]{2,1,0:T(8,128)(2,1)S(1)} %bitcast.138), channel_id=1, replica_groups=mesh['stage'=1,'data'=8] {'data'}, dimensions={0} | all-to-all | bytes 11534336 | tf_op jit(solution)/shard_map/all_to_all | solution.py:111
  1144.0 54.5 %all-gather.6.cloned.1.call-done.refs_0_ = bf16[2,2048,1408]{2,1,0:T(8,128)(2,1)} async-done(((bf16[2,256,1408]{2,1,0:T(8,128)(2,1)}), bf16[2,2048,1408]{2,1,0:T(8,128)(2,1)}) %all-gather.6.cloned.1.call-update) | async-done | bytes 11534352 | tf_op jit(solution)/shard_map/all_gather | solution.py:147
  1198.5 210.5 %all-gather.14.cloned.1.call-done.refs_0_ = bf16[8,2048,1408]{2,1,0:T(8,128)(2,1)} async-done(((bf16[8,256,1408]{2,1,0:T(8,128)(2,1)}), bf16[8,2048,1408]{2,1,0:T(8,128)(2,1)}) %all-gather.14.cloned.1.call-update) | async-done | bytes 46137360 | tf_op jit(solution)/shard_map/all_gather | solution.py:147
  1409.0 35.2 %shard_map.52.refs_1_ = bf16[32,2048,1408]{2,1,0:T(8,128)(2,1)} custom-call(bf16[8,2048,1408]{2,1,0:T(8,128)(2,1)} %all-gather.14.cloned.1.call-done.refs_0_), custom_call_target="tpu_custom_call" | custom-call | flops 46137344 | bytes 92274688 | tf_op jit(solution)/shard_map/pallas_call | solution.py:87
  1444.2 127.0 %all-gather.8.cloned.1.call-done.refs_0_ = bf16[6,2048,1408]{2,1,0:T(8,128)(2,1)} async-done(((bf16[6,256,1408]{2,1,0:T(8,128)(2,1)}), bf16[6,2048,1408]{2,1,0:T(8,128)(2,1)}) %all-gather.8.cloned.1.call-update) | async-done | bytes 34603024 | tf_op jit(solution)/shard_map/all_gather | solution.py:147
  1571.2 210.3 %all-gather.12.cloned.1.call-done.refs_0_ = bf16[8,2048,1408]{2,1,0:T(8,128)(2,1)} async-done(((bf16[8,256,1408]{2,1,0:T(8,128)(2,1)}), bf16[8,2048,1408]{2,1,0:T(8,128)(2,1)}) %all-gather.12.cloned.1.call-update) | async-done | bytes 46137360 | tf_op jit(solution)/shard_map/all_gather | solution.py:147
  1781.5 35.9 %shard_map.53.refs_1_ = bf16[32,2048,1408]{2,1,0:T(8,128)(2,1)} custom-call(bf16[8,2048,1408]{2,1,0:T(8,128)(2,1)} %all-gather.12.cloned.1.call-done.refs_0_, bf16[32,2048,1408]{2,1,0:T(8,128)(2,1)} %shard_map.52.refs_1_), custom_call_target="tpu_custom_call", output_to_operand_aliasing={{}: (1, {})} | custom-call | flops 46137344 | bytes 92274688 | tf_op jit(solution)/shard_map/pallas_call | solution.py:87
  1817.4 174.4 %all-gather.10.cloned.1.call-done.refs_0_ = bf16[8,2048,1408]{2,1,0:T(8,128)(2,1)} async-done(((bf16[8,256,1408]{2,1,0:T(8,128)(2,1)}), bf16[8,2048,1408]{2,1,0:T(8,128)(2,1)}) %all-gather.10.cloned.1.call-update) | async-done | bytes 46137360 | tf_op jit(solution)/shard_map/all_gather | solution.py:147
  1991.9 34.3 %shard_map.54.refs_1_ = bf16[32,2048,1408]{2,1,0:T(8,128)(2,1)} custom-call(bf16[8,2048,1408]{2,1,0:T(8,128)(2,1)} %all-gather.10.cloned.1.call-done.refs_0_, bf16[32,2048,1408]{2,1,0:T(8,128)(2,1)} %shard_map.53.refs_1_), custom_call_target="tpu_custom_call", output_to_operand_aliasing={{}: (1, {})} | custom-call | flops 46137344 | bytes 92274688 | tf_op jit(solution)/shard_map/pallas_call | solution.py:87
  2026.1 25.8 %shard_map.55.refs_1_ = bf16[32,2048,1408]{2,1,0:T(8,128)(2,1)} custom-call(bf16[6,2048,1408]{2,1,0:T(8,128)(2,1)} %all-gather.8.cloned.1.call-done.refs_0_, bf16[32,2048,1408]{2,1,0:T(8,128)(2,1)} %shard_map.54.refs_1_), custom_call_target="tpu_custom_call", output_to_operand_aliasing={{}: (1, {})} | custom-call | flops 34603008 | bytes 69206016 | tf_op jit(solution)/shard_map/pallas_call | solution.py:87
  (114 shorter events, 589.9 us)
Async XLA Ops:
  30.8 69.4 %all-to-all-start.1 = ((bf16[8,256,1408]{2,1,0:T(8,128)(2,1)}), bf16[8,256,1408]{2,1,0:T(8,128)(2,1)}, u32[]{:S(2)}, u32[]{:S(2)}) async-start(bf16[8,256,1408]{2,1,0:T(8,128)(2,1)} %get-tuple-element.27), calls=%async_computation.1 | async-start | bytes 11534336 | tf_op jit(solution)/shard_map/all_to_all | solution.py:111
  212.0 10.0 copy-start
  230.3 18.0 all-to-all-start.2
  248.3 69.4 %all-to-all-start.4 = ((bf16[8,256,1408]{2,1,0:T(8,128)(2,1)}), bf16[8,256,1408]{2,1,0:T(8,128)(2,1)}, u32[]{:S(2)}, u32[]{:S(2)}) async-start(bf16[8,256,1408]{2,1,0:T(8,128)(2,1)} %bitcast.136), calls=%async_computation.4 | async-start | bytes 11534336 | tf_op jit(solution)/shard_map/all_to_all | solution.py:111
  317.7 194.5 %all-to-all-start.3 = ((bf16[24,256,1408]{2,1,0:T(8,128)(2,1)}), bf16[24,256,1408]{2,1,0:T(8,128)(2,1)}, u32[]{:S(2)}, u32[]{:S(2)}) async-start(bf16[24,256,1408]{2,1,0:T(8,128)(2,1)} %get-tuple-element.29), calls=%async_computation.3 | async-start | bytes 34603008 | tf_op jit(solution)/shard_map/all_to_all | solution.py:111
  642.6 22.5 %slice-start.2 = ((s8[5767168]{0:T(1024)(128)(4,1)}), s8[4194304]{0:T(1024)(128)(4,1)S(1)}, s32[]{:S(2)}) async-start(s8[5767168]{0:T(1024)(128)(4,1)} %bitcast.143), calls=%async_computation.15 | async-start | bytes 8388608
  650.8 14.2 slice-start.3
  748.0 69.4 %all-to-all-start.5 = ((bf16[8,256,1408]{2,1,0:T(8,128)(2,1)}), bf16[8,256,1408]{2,1,0:T(8,128)(2,1)}, u32[]{:S(2)}, u32[]{:S(2)}) async-start(bf16[8,256,1408]{2,1,0:T(8,128)(2,1)} %bitcast.135), calls=%async_computation.5 | async-start | bytes 11534336 | tf_op jit(solution)/shard_map/all_to_all | solution.py:111
  751.5 20.3 slice-start.10
  764.7 7.0 slice-start.11
  828.4 20.7 %slice-start.4 = ((s8[5767168]{0:T(1024)(128)(4,1)}), s8[4194304]{0:T(1024)(128)(4,1)S(1)}, s32[]{:S(2)}) async-start(s8[5767168]{0:T(1024)(128)(4,1)} %bitcast.150), calls=%async_computation.17 | async-start | bytes 8388608
  842.1 7.0 slice-start.5
  842.1 19.0 slice-start
  849.2 12.0 slice-start.1
  944.1 69.4 %all-to-all-start.6 = ((bf16[8,256,1408]{2,1,0:T(8,128)(2,1)}), bf16[8,256,1408]{2,1,0:T(8,128)(2,1)}, u32[]{:S(2)}, u32[]{:S(2)}) async-start(bf16[8,256,1408]{2,1,0:T(8,128)(2,1)} %bitcast.134), calls=%async_computation.6 | async-start | bytes 11534336 | tf_op jit(solution)/shard_map/all_to_all | solution.py:111
  947.6 250.9 %all-gather.6.cloned.1.call-start = ((), (), s32[]{:S(2)}) async-start(), calls=%async_computation.8 | async-start | bytes 12976128 | tf_op jit(solution)/shard_map/all_gather | solution.py:147
  947.6 20.3 slice-start.8
  960.9 7.0 slice-start.9
  1024.5 20.7 %slice-start.6 = ((s8[5767168]{0:T(1024)(128)(4,1)}), s8[4194304]{0:T(1024)(128)(4,1)S(1)}, s32[]{:S(2)}) async-start(s8[5767168]{0:T(1024)(128)(4,1)} %bitcast.152), calls=%async_computation.19 | async-start | bytes 8388608
  1038.2 7.0 slice-start.7
  1137.3 271.7 %all-gather.14.cloned.1.call-start = ((), (), s32[]{:S(2)}) async-start(), calls=%async_computation.12 | async-start | bytes 51904512 | tf_op jit(solution)/shard_map/all_gather | solution.py:147
  1138.0 433.2 %all-gather.8.cloned.1.call-start = ((), (), s32[]{:S(2)}) async-start(), calls=%async_computation.9 | async-start | bytes 38928384 | tf_op jit(solution)/shard_map/all_gather | solution.py:147
  1142.8 638.7 %all-gather.12.cloned.1.call-start = ((), (), s32[]{:S(2)}) async-start(), calls=%async_computation.11 | async-start | bytes 51904512 | tf_op jit(solution)/shard_map/all_gather | solution.py:147
  1143.4 848.4 %all-gather.10.cloned.1.call-start = ((), (), s32[]{:S(2)}) async-start(), calls=%async_computation.10 | async-start | bytes 51904512 | tf_op jit(solution)/shard_map/all_gather | solution.py:147
Sparse Core Ops, SparseCore 0:
  1137.4 61.0 all-gather.5
  1200.4 208.5 all-gather.13
  1410.8 160.3 all-gather.7
  1572.9 208.5 all-gather.11
  1783.2 208.5 all-gather.9

commit v2 on v1

v2 whole, which is shorter than its diff:
```python
import math
import jax
import jax.numpy as jnp
from jax import lax
from jax.experimental import pallas as pl
from jax.experimental.pallas import tpu as pltpu
from jax.sharding import PartitionSpec as P

NS_ITERS = 5
MOMENTUM = 0.95
LEARN_RATE = 0.02
WEIGHT_DECAY = 0.1
NORM_EPS = 1e-7
COEF_A = 3.4445
COEF_B = -4.7750
COEF_C = 2.0315

AGENDA = (
    ("ns", 0, 0), ("ns", 0, 1), ("ns", 0, 2), ("ns", 0, 3), ("ns", 0, 4), ("out", 0),
    ("ns", 1, 0), ("ns", 1, 1), ("upd", 0), ("ns", 1, 2), ("ns", 1, 3), ("ns", 1, 4), ("out", 1),
    ("ns", 2, 0), ("dg", 0), ("pp", 0, 1, 0), ("pp", 0, 2, 1), ("ns", 2, 1), ("ns", 2, 2), ("pp", 0, 1, 1), ("pp", 0, 2, 0), ("ns", 2, 3), ("ns", 2, 4),
    ("upd", 1), ("out", 2), ("ns", 3, 0), ("ns", 3, 1), ("ns", 3, 2), ("pp", 0, 3, 0), ("pp", 0, 3, 1), ("ns", 3, 3), ("upd", 2), ("ns", 3, 4), ("out", 3),
    ("pl", 0, 0, 0), ("pl", 0, 0, 1), ("pl", 0, 1, 0), ("pl", 0, 1, 1), ("pl", 0, 2, 0), ("pl", 0, 2, 1), ("pl", 0, 3, 0), ("pl", 0, 3, 1),
    ("dg", 1), ("pp", 1, 1, 0), ("pp", 1, 2, 1), ("pl", 1, 0, 0), ("pl", 1, 0, 1), ("pl", 1, 1, 0),
    ("pp", 1, 1, 1), ("pp", 1, 2, 0), ("pl", 1, 2, 1), ("pl", 1, 1, 1), ("pl", 1, 2, 0),
    ("upd", 3), ("pl", 2, 0, 0), ("dg", 2), ("pp", 2, 1, 0), ("pp", 2, 2, 1), ("pl", 2, 0, 1), ("pl", 2, 1, 0),
    ("pp", 2, 1, 1), ("pp", 2, 2, 0), ("pl", 2, 2, 1), ("pl", 2, 1, 1), ("pl", 2, 2, 0),
    ("pp", 1, 3, 0), ("pp", 1, 3, 1), ("pl", 3, 0, 0), ("pl", 1, 3, 0), ("pl", 1, 3, 1),
    ("dg", 3), ("pp", 3, 1, 0), ("pp", 3, 2, 1), ("pl", 3, 0, 1), ("pl", 3, 1, 0),
    ("pp", 3, 1, 1), ("pp", 3, 2, 0), ("pl", 3, 2, 1), ("pl", 3, 1, 1), ("pl", 3, 2, 0),
    ("pp", 2, 3, 0), ("pp", 2, 3, 1), ("pl", 2, 3, 0), ("pl", 2, 3, 1),
    ("pp", 3, 3, 0), ("pp", 3, 3, 1), ("pl", 3, 3, 0), ("pl", 3, 3, 1),
)


def after(value, *deps):
    return lax.optimization_barrier((value, *deps))[0]


def ns_step(x_mat):
    wide = x_mat.shape[0] <= x_mat.shape[1]
    eq = "ip,jp->ij" if wide else "pi,pj->ij"
    gram_mat = jnp.einsum(eq, x_mat, x_mat, preferred_element_type=jnp.float32).astype(jnp.bfloat16)
    square = jnp.dot(gram_mat, gram_mat, preferred_element_type=jnp.float32)
    poly_mat = (COEF_B * gram_mat.astype(jnp.float32) + COEF_C * square).astype(jnp.bfloat16)
    poly_mat = lax.optimization_barrier(poly_mat)
    eq = "ij,jp->ip" if wide else "ij,pj->pi"
    prod_mat = jnp.einsum(eq, poly_mat, x_mat, preferred_element_type=jnp.float32)
    return (COEF_A * x_mat.astype(jnp.float32) + prod_mat).astype(jnp.bfloat16)


def momentum_body(me_ref, mom_ref, grad_ref, *refs):
    new_ref, low_ref, sum_ref = refs[-3:]
    new = MOMENTUM * mom_ref[...] + grad_ref[...].astype(jnp.float32)
    new_ref[...] = new
    low_ref[...] = new.astype(jnp.bfloat16)
    sum_ref[...] = jnp.broadcast_to(jnp.sum(new * new), sum_ref.shape)


def momentum_rows(me, mom_rows, grad_rows, whole, first, waves, group, by_distance):
    total, rows, cols = mom_rows.shape
    here = pl.BlockSpec((1, rows, cols), lambda k, d, me_ref: (first + k * group + d, 0, 0))
    in_specs, operands, aliases = [here, here], [mom_rows, grad_rows], {}
    if whole is not None:
        in_specs.append(pl.BlockSpec(memory_space=pl.ANY))
        operands.append(whole)
        aliases = {3: 0}
    count = waves * group
    if by_distance:
        low_map = lambda k, d, me_ref: (lax.bitwise_xor(d, me_ref[0]), 0, 0)
    else:
        low_map = lambda k, d, me_ref: (d * waves + k, 0, 0)
    return pl.pallas_call(
        momentum_body,
        grid_spec=pltpu.PrefetchScalarGridSpec(
            num_scalar_prefetch=1,
            grid=(waves, group),
            in_specs=in_specs,
            out_specs=(
                here,
                pl.BlockSpec((1, rows, cols), low_map),
                pl.BlockSpec((1, 8, 128), lambda k, d, me_ref: (d * waves + k, 0, 0)),
            ),
        ),
        out_shape=(
            jax.ShapeDtypeStruct((total, rows, cols), jnp.float32),
            jax.ShapeDtypeStruct((count, rows, cols), jnp.bfloat16),
            jax.ShapeDtypeStruct((count, 8, 128), jnp.float32),
        ),
        input_output_aliases=aliases,
        cost_estimate=pl.CostEstimate(flops=4 * count * rows * cols, bytes_accessed=12 * count * rows * cols, transcendentals=0),
    )(me, *operands)


def normalize_body(me_ref, norm_ref, *refs):
    out_ref = refs[-1]
    rows = refs[0].shape[1]
    for distance, piece in enumerate(refs[:-1]):
        start = pl.multiple_of(lax.bitwise_xor(me_ref[0], distance) * rows, rows)
        out_ref[pl.ds(start, rows)] = (piece[0].astype(jnp.float32) / norm_ref[0]).astype(jnp.bfloat16)


def normalize(me, norm, pieces):
    _, rows, cols = pieces[0].shape
    return pl.pallas_call(
        normalize_body,
        in_specs=[pl.BlockSpec(memory_space=pltpu.SMEM)] * 2 + [pl.BlockSpec(memory_space=pltpu.VMEM)] * len(pieces),
        out_specs=pl.BlockSpec(memory_space=pltpu.VMEM),
        out_shape=jax.ShapeDtypeStruct((rows * len(pieces), cols), jnp.bfloat16),
        cost_estimate=pl.CostEstimate(flops=8 * rows * cols, bytes_accessed=32 * rows * cols, transcendentals=0),
    )(me, norm, *pieces)


def place_body(me_ref, even_ref, odd_ref, *refs):
    out_ref = refs[-1]
    rows = even_ref.shape[1]
    swap = lax.rem(me_ref[0], 2)
    out_ref[0, pl.ds(pl.multiple_of(swap * rows, rows), rows)] = even_ref[0]
    out_ref[0, pl.ds(pl.multiple_of((1 - swap) * rows, rows), rows)] = odd_ref[0]


def place(whole, me, even, odd, pair, first, total, group):
    mats, rows, cols = even.shape
    piece = pl.BlockSpec((1, rows, cols), lambda i, me_ref: (i, 0, 0))
    in_specs, operands, aliases = [piece, piece], [even, odd], {}
    if whole is not None:
        in_specs.append(pl.BlockSpec(memory_space=pl.ANY))
        operands.append(whole)
        aliases = {3: 0}
    return pl.pallas_call(
        place_body,
        grid_spec=pltpu.PrefetchScalarGridSpec(
            num_scalar_prefetch=1,
            grid=(mats,),
            in_specs=in_specs,
            out_specs=pl.BlockSpec((1, 2 * rows, cols), lambda i, me_ref: (i + first, lax.bitwise_xor(me_ref[0] // 2, pair), 0)),
        ),
        out_shape=jax.ShapeDtypeStruct((total, rows * group, cols), even.dtype),
        input_output_aliases=aliases,
        cost_estimate=pl.CostEstimate(flops=4 * even.size, bytes_accessed=8 * even.size, transcendentals=0),
    )(me, *operands)


def solution(mesh):
    group = mesh.shape["data"]
    row_spec = P("stage", "data", None)
    full_spec = P("stage", None, None)

    def local_step(w_rows, mom_rows, grad_rows):
        mat_count, rows_dev, col_count = mom_rows.shape
        waves = mat_count // group
        rows_all = rows_dev * group
        rms_scale = 0.2 * math.sqrt(max(rows_all, col_count))

        def exchange(array):
            return lax.all_to_all(array, "data", 0, 0, tiled=True)

        def hop(array, bit):
            return lax.ppermute(array, "data", [(i, i ^ bit) for i in range(group)])

        my_index = lax.axis_index("data")
        me = my_index.astype(jnp.int32).reshape(1)
        mom_new, low_0, sum_0 = momentum_rows(me, mom_rows, grad_rows, None, 0, 1, group, False)
        mom_new, low_1, sum_1 = momentum_rows(me, mom_rows, grad_rows, mom_new, group, 2, group, False)
        mom_new, low_3, sum_3 = momentum_rows(me, mom_rows, grad_rows, mom_new, 3 * group, 1, group, True)
        part = jnp.concatenate([sum_0[:, 0, 0], sum_1[:, 0, 0], sum_3[:, 0, 0]])
        sq_total = part
        for bit in range(1, group):
            sq_total = sq_total + hop(part, bit)
        low_0 = exchange(low_0)
        low_1 = exchange(after(low_1, low_0)).reshape(group, 2, rows_dev, col_count)
        low_3 = lax.optimization_barrier(tuple(lax.slice_in_dim(low_3, r, r + 1) for r in range(group)))
        low_3 = [low_3[0]] + [hop(low_3[r], r) for r in range(1, group)]

        def begin(wave):
            place_of = (my_index, group + 2 * my_index, group + 2 * my_index + 1, 3 * group + my_index)[wave]
            norm = jnp.sqrt(lax.dynamic_slice_in_dim(sq_total, place_of, 1)) + NORM_EPS
            if wave == 3:
                return normalize(me, norm, after(tuple(low_3), state["x"]))
            low = low_0 if wave == 0 else low_1[:, wave - 1]
            return (low.reshape(rows_all, col_count).astype(jnp.float32) / norm).astype(jnp.bfloat16)

        half = group // 2

        def update(ortho, wave):
            halves = []
            for h in range(2):
                w_old = lax.slice_in_dim(w_rows, wave * group + h * half, wave * group + (h + 1) * half)
                part = lax.slice_in_dim(ortho, h * half, (h + 1) * half)
                w_new = w_old - LEARN_RATE * (part.astype(jnp.float32) * rms_scale + WEIGHT_DECAY * w_old)
                halves.append(w_new.astype(jnp.bfloat16))
            return lax.optimization_barrier(tuple(halves))

        got = {(w, h): {} for w in range(waves) for h in range(2)}
        final = {}
        state = {"x": None, "params": None}
        outs = {}

        def tie(*arrays):
            key = "x" if state["params"] is None else "params"
            state[key], *arrays = lax.optimization_barrier((state[key], *arrays))
            return arrays

        for kind, wave, *where in AGENDA:
            if kind == "ns":
                if where[0] == 0:
                    state["x"] = begin(wave) if state["x"] is None else after(begin(wave), state["x"])
                state["x"] = lax.optimization_barrier(ns_step(state["x"]))
            elif kind == "out":
                outs[wave] = exchange(final[wave].reshape(group, rows_dev, col_count))
            elif kind == "upd":
                (ortho,) = tie(outs.pop(wave))
                for h, own in enumerate(tie(*update(ortho, wave))):
                    mine = got[wave, h]
                    mine[0] = own
                    mine[1] = hop(own, 1)
                    mine[2] = hop(own, 2)
                    mine[4] = hop(own, 4)
            elif kind == "dg":
                got[wave, 0][2], got[wave, 1][4] = tie(got[wave, 0][2], got[wave, 1][4])
                got[wave, 0][6] = hop(got[wave, 0][2], 4)
                got[wave, 1][6] = hop(got[wave, 1][4], 2)
            elif kind == "pp":
                pair, h = where
                mine = got[wave, h]
                (mine[2 * pair],) = tie(mine[2 * pair])
                mine[2 * pair + 1] = hop(mine[2 * pair], 1)
            else:
                pair, h = where
                mine = got[wave, h]
                even = mine[2 * pair]
                if state["params"] is None:
                    even = after(even, state["x"])
                state["params"] = place(
                    state["params"], me, even, mine[2 * pair + 1], pair, wave * group + h * half, mat_count, group
                )
            if kind == "ns" and where[0] == NS_ITERS - 1:
                final[wave] = state["x"]
        params = state["params"]
        return params, mom_new

    return jax.shard_map(local_step, mesh=mesh, in_specs=(row_spec, row_spec, row_spec), out_specs=(full_spec, row_spec), check_vma=False)
```

time: 2080 us -> 1660 us (0.80)
  waiting for transfers between devices: 1110 us -> 672 us
  blocking collectives: 77.1 us -> 0 us
  starting transfers between devices: 21 us -> 82.1 us
  Pallas kernels: 197 us -> 242 us
    all_gather x5 -> x0, waiting for transfers between devices: 777 us -> none  [local_step(): lax.all_gather(part, 'data', axis=1, tiled=True)]
    ppermute x0 -> x70, waiting for transfers between devices: none -> 575 us  [hop(): return lax.ppermute(array, 'data', [(i, i ^ bit) for i in range(group)])]
    all_to_all x6, waiting for transfers between devices: 331 us -> 97.4 us  [exchange(): return lax.all_to_all(array, 'data', 0, 0, tiled=True)]
    all_to_all x2 -> x0, blocking collectives: 77.1 us -> none  [exchange(): return lax.all_to_all(array, 'data', 0, 0, tiled=True)]
    ppermute x0 -> x70, starting transfers between devices: none -> 59 us  [hop(): return lax.ppermute(array, 'data', [(i, i ^ bit) for i in range(group)])]
    pallas_call x7 -> x36, Pallas kernels: 197 us -> 242 us  [the longest x32 179 us: place(): pl.pallas_call(place_body, grid_spec=pltpu.PrefetchScalarGridSpec(num_sca...]
  transfers between devices with their start and end apart: 11 -> 76, of which waited for: 10 -> 27; matrix products, arithmetic and copies ran while one was open for 5% -> 38% of each run, Pallas kernels for 5% -> 14%
where the time goes in v2:
time: 1660 us; the launch traced here: 1650 us
  waiting for transfers between devices  672 us (40%)
  matrix products  569 us (34%)
  Pallas kernels  242 us (15%)
  starting transfers between devices  82.1 us (5%)
  other arithmetic  50.2 us (3%)
  local copies, waits for them, and re-layouts  25.8 us (2%)
    ppermute x70, waiting for transfers between devices, hop(): return lax.ppermute(array, 'data', [(i, i ^ bit) for i in range(group)])  575 us
    dot_general x20, matrix products, ns_step(): jnp.einsum(eq, poly_mat, x_mat, preferred_element_type=jnp.float32)  219 us
    dot_general x20, matrix products, ns_step(): jnp.einsum(eq, x_mat, x_mat, preferred_element_type=jnp.float32)  209 us
    pallas_call x32, Pallas kernels, place(): pl.pallas_call(place_body, grid_spec=pltpu.PrefetchScalarGridSpec(num_sca...  179 us
    dot_general x20, matrix products, ns_step(): square = jnp.dot(gram_mat, gram_mat, preferred_element_type=jnp.float32)  141 us
    all_to_all x6, waiting for transfers between devices, exchange(): return lax.all_to_all(array, 'data', 0, 0, tiled=True)  97.4 us
    ppermute x70, starting transfers between devices, hop(): return lax.ppermute(array, 'data', [(i, i ^ bit) for i in range(group)])  59 us
    pallas_call x3, Pallas kernels, momentum_rows(): pl.pallas_call(momentum_body, grid_spec=pltpu.PrefetchScalarGridSpec(num_...  57.6 us
  transfers between devices with their start and end apart: 76, of which 27 were waited for; matrix products, arithmetic and copies ran while one was open for 38% of the time, Pallas kernels for 14%

profile of v2, /device:TPU:0, one launch (start us, length us, event | category | flops | bytes accessed | tf_op | source)
XLA Modules:
  0.0 1646.1 jit_solution(11376767005683182910)
XLA Ops:
  0.6 14.6 shard_map.50
  19.5 28.4 %shard_map.51 = (f32[32,256,1408]{2,1,0:T(8,128)}, bf16[16,256,1408]{2,1,0:T(8,128)(2,1)}, f32[16,8,128]{2,1,0:T(8,128)}) custom-call(s32[1]{0:T(128)} %bitcast.me_ref, f32[32,256,1408]{2,1,0:T(8,128)} %mom_ref.5, bf16[32,256,1408]{2,1,0:T(8,128)(2,1)} %grad_ref.5, f32[32,256,1408]{2,1,0:T(8,128)} %get-tuple-element.121.refs_0_), custom_call_target="tpu_custom_call", output_to_operand_aliasing={{0}: (3, {})} | custom-call | flops 23068672 | bytes 69206016 | tf_op jit(solution)/shard_map/pallas_call | solution.py:73
  47.9 14.6 shard_map.52
  183.0 13.2 convolution_convert_fusion.16
  242.1 68.6 %all-to-all-done.1 = bf16[16,256,1408]{2,1,0:T(8,128)(2,1)} async-done(((bf16[16,256,1408]{2,1,0:T(8,128)(2,1)}), bf16[16,256,1408]{2,1,0:T(8,128)(2,1)}, u32[]{:S(2)}, u32[]{:S(2)}) %all-to-all-start.1) | async-done | bytes 11534368 | tf_op jit(solution)/shard_map/all_to_all | solution.py:156
  462.6 14.0 add_convert_fusion.10
  510.8 41.5 %collective-permute-done.14.even_ref = bf16[4,256,1408]{2,1,0:T(8,128)(2,1)} collective-permute-done((bf16[4,256,1408]{2,1,0:T(8,128)(2,1)}, bf16[4,256,1408]{2,1,0:T(8,128)(2,1)}, u32[]{:S(2)}, u32[]{:S(2)}) %collective-permute-start.14) | collective-permute-done | bytes 2883616 | tf_op jit(solution)/shard_map/ppermute | solution.py:159
  553.9 13.7 convolution_convert_fusion.8
  611.7 62.1 %collective-permute-done.16.even_ref = bf16[4,256,1408]{2,1,0:T(8,128)(2,1)} collective-permute-done((bf16[4,256,1408]{2,1,0:T(8,128)(2,1)}, bf16[4,256,1408]{2,1,0:T(8,128)(2,1)}, u32[]{:S(2)}, u32[]{:S(2)}) %collective-permute-start.16) | collective-permute-done | bytes 2883616 | tf_op jit(solution)/shard_map/ppermute | solution.py:159
  749.6 67.4 %collective-permute-done.8.refs_2_ = bf16[1,256,1408]{2,1,0:T(8,128)(2,1)S(1)} collective-permute-done((bf16[1,256,1408]{2,1,0:T(8,128)(2,1)}, bf16[1,256,1408]{2,1,0:T(8,128)(2,1)S(1)}, u32[]{:S(2)}, u32[]{:S(2)}) %collective-permute-start.8) | collective-permute-done | bytes 720928 | tf_op jit(solution)/shard_map/ppermute | solution.py:159
  817.8 13.5 collective-permute-done.9.refs_3_
  839.6 13.7 convolution_convert_fusion.4
  942.2 12.0 add_convert_fusion.1
  985.7 12.0 add_convert_fusion
  1065.6 43.1 %collective-permute-done.34.even_ref = bf16[4,256,1408]{2,1,0:T(8,128)(2,1)} collective-permute-done((bf16[4,256,1408]{2,1,0:T(8,128)(2,1)}, bf16[4,256,1408]{2,1,0:T(8,128)(2,1)}, u32[]{:S(2)}, u32[]{:S(2)}) %collective-permute-start.34) | collective-permute-done | bytes 2883616 | tf_op jit(solution)/shard_map/ppermute | solution.py:159
  1110.6 16.0 collective-permute-start.39
  1145.0 26.9 %all-to-all-done.5 = bf16[8,256,1408]{2,1,0:T(8,128)(2,1)} async-done(((bf16[8,256,1408]{2,1,0:T(8,128)(2,1)}), bf16[8,256,1408]{2,1,0:T(8,128)(2,1)}, u32[]{:S(2)}, u32[]{:S(2)}) %all-to-all-start.5) | async-done | bytes 5767200 | tf_op jit(solution)/shard_map/all_to_all | solution.py:156
  1186.9 45.0 %collective-permute-done.39.even_ref = bf16[4,256,1408]{2,1,0:T(8,128)(2,1)} collective-permute-done((bf16[4,256,1408]{2,1,0:T(8,128)(2,1)}, bf16[4,256,1408]{2,1,0:T(8,128)(2,1)}, u32[]{:S(2)}, u32[]{:S(2)}) %collective-permute-start.39) | collective-permute-done | bytes 2883616 | tf_op jit(solution)/shard_map/ppermute | solution.py:159
  1246.6 51.6 %collective-permute-done.43.even_ref = bf16[4,256,1408]{2,1,0:T(8,128)(2,1)} collective-permute-done((bf16[4,256,1408]{2,1,0:T(8,128)(2,1)}, bf16[4,256,1408]{2,1,0:T(8,128)(2,1)}, u32[]{:S(2)}, u32[]{:S(2)}) %collective-permute-start.43) | collective-permute-done | bytes 2883616 | tf_op jit(solution)/shard_map/ppermute | solution.py:159
  1318.8 44.8 %collective-permute-done.48.even_ref = bf16[4,256,1408]{2,1,0:T(8,128)(2,1)} collective-permute-done((bf16[4,256,1408]{2,1,0:T(8,128)(2,1)}, bf16[4,256,1408]{2,1,0:T(8,128)(2,1)}, u32[]{:S(2)}, u32[]{:S(2)}) %collective-permute-start.48) | collective-permute-done | bytes 2883616 | tf_op jit(solution)/shard_map/ppermute | solution.py:159
  1385.2 43.7 %collective-permute-done.53.even_ref = bf16[4,256,1408]{2,1,0:T(8,128)(2,1)} collective-permute-done((bf16[4,256,1408]{2,1,0:T(8,128)(2,1)}, bf16[4,256,1408]{2,1,0:T(8,128)(2,1)}, u32[]{:S(2)}, u32[]{:S(2)}) %collective-permute-start.53) | collective-permute-done | bytes 2883616 | tf_op jit(solution)/shard_map/ppermute | solution.py:159
  1445.2 50.3 %collective-permute-done.57.even_ref = bf16[4,256,1408]{2,1,0:T(8,128)(2,1)} collective-permute-done((bf16[4,256,1408]{2,1,0:T(8,128)(2,1)}, bf16[4,256,1408]{2,1,0:T(8,128)(2,1)}, u32[]{:S(2)}, u32[]{:S(2)}) %collective-permute-start.57) | collective-permute-done | bytes 2883616 | tf_op jit(solution)/shard_map/ppermute | solution.py:159
  1517.2 43.6 %collective-permute-done.62.even_ref = bf16[4,256,1408]{2,1,0:T(8,128)(2,1)} collective-permute-done((bf16[4,256,1408]{2,1,0:T(8,128)(2,1)}, bf16[4,256,1408]{2,1,0:T(8,128)(2,1)}, u32[]{:S(2)}, u32[]{:S(2)}) %collective-permute-start.62) | collective-permute-done | bytes 2883616 | tf_op jit(solution)/shard_map/ppermute | solution.py:159
  1579.0 48.4 %collective-permute-done.66.even_ref = bf16[4,256,1408]{2,1,0:T(8,128)(2,1)} collective-permute-done((bf16[4,256,1408]{2,1,0:T(8,128)(2,1)}, bf16[4,256,1408]{2,1,0:T(8,128)(2,1)}, u32[]{:S(2)}, u32[]{:S(2)}) %collective-permute-start.66) | collective-permute-done | bytes 2883616 | tf_op jit(solution)/shard_map/ppermute | solution.py:159
  (289 shorter events, 839.0 us)
Async XLA Ops:
  15.2 77.1 %all-to-all-start = ((bf16[8,256,1408]{2,1,0:T(8,128)(2,1)}), bf16[8,256,1408]{2,1,0:T(8,128)(2,1)}, u32[]{:S(2)}, u32[]{:S(2)}) async-start(bf16[8,256,1408]{2,1,0:T(8,128)(2,1)} %get-tuple-element.135), calls=%async_computation | async-start | bytes 11534336 | tf_op jit(solution)/shard_map/all_to_all | solution.py:156
  85.2 650.8 %collective-permute-start.10 = (bf16[1,256,1408]{2,1,0:T(8,128)(2,1)}, bf16[1,256,1408]{2,1,0:T(8,128)(2,1)}, u32[]{:S(2)}, u32[]{:S(2)}) collective-permute-start(bf16[1,256,1408]{2,1,0:T(8,128)(2,1)} %get-tuple-element.130), channel_id=1, source_target_pairs={{0,4},{1,5},{2,6},{3,7},{4,0},{5,1},{6,2},{7,3}} | collective-permute-start | bytes 2162696 | tf_op jit(solution)/shard_map/ppermute | solution.py:159
  86.1 651.9 %collective-permute-start.11 = (bf16[1,256,1408]{2,1,0:T(8,128)(2,1)}, bf16[1,256,1408]{2,1,0:T(8,128)(2,1)}, u32[]{:S(2)}, u32[]{:S(2)}) collective-permute-start(bf16[1,256,1408]{2,1,0:T(8,128)(2,1)} %get-tuple-element.131), channel_id=1, source_target_pairs={{0,5},{1,4},{2,7},{3,6},{4,1},{5,0},{6,3},{7,2}} | collective-permute-start | bytes 2162696 | tf_op jit(solution)/shard_map/ppermute | solution.py:159
  87.7 659.6 %collective-permute-start.12 = (bf16[1,256,1408]{2,1,0:T(8,128)(2,1)}, bf16[1,256,1408]{2,1,0:T(8,128)(2,1)}, u32[]{:S(2)}, u32[]{:S(2)}) collective-permute-start(bf16[1,256,1408]{2,1,0:T(8,128)(2,1)} %get-tuple-element.132), channel_id=1, source_target_pairs={{0,6},{1,7},{2,4},{3,5},{4,2},{5,3},{6,0},{7,1}} | collective-permute-start | bytes 2162696 | tf_op jit(solution)/shard_map/ppermute | solution.py:159
  178.9 131.9 %all-to-all-start.1 = ((bf16[16,256,1408]{2,1,0:T(8,128)(2,1)}), bf16[16,256,1408]{2,1,0:T(8,128)(2,1)}, u32[]{:S(2)}, u32[]{:S(2)}) async-start(bf16[16,256,1408]{2,1,0:T(8,128)(2,1)} %get-tuple-element.136), calls=%async_computation.1 | async-start | bytes 23068672 | tf_op jit(solution)/shard_map/all_to_all | solution.py:156
  507.0 225.4 %all-to-all-start.3 = ((bf16[8,256,1408]{2,1,0:T(8,128)(2,1)}), bf16[8,256,1408]{2,1,0:T(8,128)(2,1)}, u32[]{:S(2)}, u32[]{:S(2)}) async-start(bf16[8,256,1408]{2,1,0:T(8,128)(2,1)} %bitcast.146), calls=%async_computation.3 | async-start | bytes 11534336 | tf_op jit(solution)/shard_map/all_to_all | solution.py:156
  552.3 121.5 %collective-permute-start.16 = (bf16[4,256,1408]{2,1,0:T(8,128)(2,1)}, bf16[4,256,1408]{2,1,0:T(8,128)(2,1)}, u32[]{:S(2)}, u32[]{:S(2)}) collective-permute-start(bf16[4,256,1408]{2,1,0:T(8,128)(2,1)} %get-tuple-element.145.even_ref), channel_id=1, source_target_pairs={{0,2},{1,3},{2,0},{3,1},{4,6},{5,7},{6,4},{7,5}} | collective-permute-start | bytes 8650760 | tf_op jit(solution)/shard_map/ppermute | solution.py:159
  552.8 122.4 %collective-permute-start.17 = (bf16[4,256,1408]{2,1,0:T(8,128)(2,1)}, bf16[4,256,1408]{2,1,0:T(8,128)(2,1)}, u32[]{:S(2)}, u32[]{:S(2)}) collective-permute-start(bf16[4,256,1408]{2,1,0:T(8,128)(2,1)} %get-tuple-element.181.even_ref), channel_id=1, source_target_pairs={{0,4},{1,5},{2,6},{3,7},{4,0},{5,1},{6,2},{7,3}} | collective-permute-start | bytes 8650760 | tf_op jit(solution)/shard_map/ppermute | solution.py:159
  673.8 73.7 %collective-permute-start.13 = (bf16[1,256,1408]{2,1,0:T(8,128)(2,1)}, bf16[1,256,1408]{2,1,0:T(8,128)(2,1)}, u32[]{:S(2)}, u32[]{:S(2)}) collective-permute-start(bf16[1,256,1408]{2,1,0:T(8,128)(2,1)} %get-tuple-element.133), channel_id=1, source_target_pairs={{0,7},{1,6},{2,5},{3,4},{4,3},{5,2},{6,1},{7,0}} | collective-permute-start | bytes 2162696 | tf_op jit(solution)/shard_map/ppermute | solution.py:159
  675.2 72.7 %collective-permute-start.7 = (bf16[1,256,1408]{2,1,0:T(8,128)(2,1)}, bf16[1,256,1408]{2,1,0:T(8,128)(2,1)}, u32[]{:S(2)}, u32[]{:S(2)}) collective-permute-start(bf16[1,256,1408]{2,1,0:T(8,128)(2,1)} %get-tuple-element.127), channel_id=1, source_target_pairs={{0,1},{1,0},{2,3},{3,2},{4,5},{5,4},{6,7},{7,6}} | collective-permute-start | bytes 2162696 | tf_op jit(solution)/shard_map/ppermute | solution.py:159
  732.4 221.8 %all-to-all-start.4 = ((bf16[8,256,1408]{2,1,0:T(8,128)(2,1)}), bf16[8,256,1408]{2,1,0:T(8,128)(2,1)}, u32[]{:S(2)}, u32[]{:S(2)}) async-start(bf16[8,256,1408]{2,1,0:T(8,128)(2,1)} %bitcast.145), calls=%async_computation.4 | async-start | bytes 11534336 | tf_op jit(solution)/shard_map/all_to_all | solution.py:156
  736.0 80.9 %collective-permute-start.8 = (bf16[1,256,1408]{2,1,0:T(8,128)(2,1)}, bf16[1,256,1408]{2,1,0:T(8,128)(2,1)S(1)}, u32[]{:S(2)}, u32[]{:S(2)}) collective-permute-start(bf16[1,256,1408]{2,1,0:T(8,128)(2,1)} %get-tuple-element.128), channel_id=1, source_target_pairs={{0,2},{1,3},{2,0},{3,1},{4,6},{5,7},{6,4},{7,5}} | collective-permute-start | bytes 2162696 | tf_op jit(solution)/shard_map/ppermute | solution.py:159
  738.0 93.3 %collective-permute-start.9 = (bf16[1,256,1408]{2,1,0:T(8,128)(2,1)}, bf16[1,256,1408]{2,1,0:T(8,128)(2,1)S(1)}, u32[]{:S(2)}, u32[]{:S(2)}) collective-permute-start(bf16[1,256,1408]{2,1,0:T(8,128)(2,1)} %get-tuple-element.129), channel_id=1, source_target_pairs={{0,3},{1,2},{2,1},{3,0},{4,7},{5,6},{6,5},{7,4}} | collective-permute-start | bytes 2162696 | tf_op jit(solution)/shard_map/ppermute | solution.py:159
  747.4 216.4 %collective-permute-start.28 = (bf16[4,256,1408]{2,1,0:T(8,128)(2,1)}, bf16[4,256,1408]{2,1,0:T(8,128)(2,1)}, u32[]{:S(2)}, u32[]{:S(2)}) collective-permute-start(bf16[4,256,1408]{2,1,0:T(8,128)(2,1)} %get-tuple-element.181.even_ref), channel_id=1, source_target_pairs={{0,1},{1,0},{2,3},{3,2},{4,5},{5,4},{6,7},{7,6}} | collective-permute-start | bytes 8650760 | tf_op jit(solution)/shard_map/ppermute | solution.py:159
  747.6 226.9 %collective-permute-start.27 = (bf16[4,256,1408]{2,1,0:T(8,128)(2,1)}, bf16[4,256,1408]{2,1,0:T(8,128)(2,1)}, u32[]{:S(2)}, u32[]{:S(2)}) collective-permute-start(bf16[4,256,1408]{2,1,0:T(8,128)(2,1)} %get-tuple-element.145.even_ref), channel_id=1, source_target_pairs={{0,1},{1,0},{2,3},{3,2},{4,5},{5,4},{6,7},{7,6}} | collective-permute-start | bytes 8650760 | tf_op jit(solution)/shard_map/ppermute | solution.py:159
  747.9 176.9 %collective-permute-start.18 = (bf16[4,256,1408]{2,1,0:T(8,128)(2,1)}, bf16[4,256,1408]{2,1,0:T(8,128)(2,1)}, u32[]{:S(2)}, u32[]{:S(2)}) collective-permute-start(bf16[4,256,1408]{2,1,0:T(8,128)(2,1)} %collective-permute-done.14.even_ref), channel_id=1, source_target_pairs={{0,4},{1,5},{2,6},{3,7},{4,0},{5,1},{6,2},{7,3}} | collective-permute-start | bytes 8650760 | tf_op jit(solution)/shard_map/ppermute | solution.py:159
  817.0 107.9 %collective-permute-start.19 = (bf16[4,256,1408]{2,1,0:T(8,128)(2,1)S(1)}, bf16[4,256,1408]{2,1,0:T(8,128)(2,1)}, u32[]{:S(2)}, u32[]{:S(2)}) collective-permute-start(bf16[4,256,1408]{2,1,0:T(8,128)(2,1)S(1)} %copy-done.1), channel_id=1, source_target_pairs={{0,2},{1,3},{2,0},{3,1},{4,6},{5,7},{6,4},{7,5}} | collective-permute-start | bytes 8650760 | tf_op jit(solution)/shard_map/ppermute | solution.py:159
  832.2 142.4 %collective-permute-start.26 = (bf16[4,256,1408]{2,1,0:T(8,128)(2,1)}, bf16[4,256,1408]{2,1,0:T(8,128)(2,1)}, u32[]{:S(2)}, u32[]{:S(2)}) collective-permute-start(bf16[4,256,1408]{2,1,0:T(8,128)(2,1)} %collective-permute-done.14.even_ref), channel_id=1, source_target_pairs={{0,1},{1,0},{2,3},{3,2},{4,5},{5,4},{6,7},{7,6}} | collective-permute-start | bytes 8650760 | tf_op jit(solution)/shard_map/ppermute | solution.py:159
  1045.0 126.9 %all-to-all-start.5 = ((bf16[8,256,1408]{2,1,0:T(8,128)(2,1)}), bf16[8,256,1408]{2,1,0:T(8,128)(2,1)}, u32[]{:S(2)}, u32[]{:S(2)}) async-start(bf16[8,256,1408]{2,1,0:T(8,128)(2,1)} %bitcast.144), calls=%async_computation.5 | async-start | bytes 11534336 | tf_op jit(solution)/shard_map/all_to_all | solution.py:156
  1048.4 78.2 %collective-permute-start.38 = (bf16[4,256,1408]{2,1,0:T(8,128)(2,1)}, bf16[4,256,1408]{2,1,0:T(8,128)(2,1)}, u32[]{:S(2)}, u32[]{:S(2)}) collective-permute-start(bf16[4,256,1408]{2,1,0:T(8,128)(2,1)} %collective-permute-done.30.even_ref), channel_id=1, source_target_pairs={{0,1},{1,0},{2,3},{3,2},{4,5},{5,4},{6,7},{7,6}} | collective-permute-start | bytes 8650760 | tf_op jit(solution)/shard_map/ppermute | solution.py:159
  1110.1 71.2 %collective-permute-start.20 = (bf16[4,256,1408]{2,1,0:T(8,128)(2,1)}, bf16[4,256,1408]{2,1,0:T(8,128)(2,1)}, u32[]{:S(2)}, u32[]{:S(2)}) collective-permute-start(bf16[4,256,1408]{2,1,0:T(8,128)(2,1)} %get-tuple-element.173.even_ref), channel_id=1, source_target_pairs={{0,1},{1,0},{2,3},{3,2},{4,5},{5,4},{6,7},{7,6}} | collective-permute-start | bytes 8650760 | tf_op jit(solution)/shard_map/ppermute | solution.py:159
  1110.6 121.2 %collective-permute-start.39 = (bf16[4,256,1408]{2,1,0:T(8,128)(2,1)}, bf16[4,256,1408]{2,1,0:T(8,128)(2,1)}, u32[]{:S(2)}, u32[]{:S(2)}) collective-permute-start(bf16[4,256,1408]{2,1,0:T(8,128)(2,1)} %get-tuple-element.173.even_ref), channel_id=1, source_target_pairs={{0,2},{1,3},{2,0},{3,1},{4,6},{5,7},{6,4},{7,5}} | collective-permute-start | bytes 8650760 | tf_op jit(solution)/shard_map/ppermute | solution.py:159
  1126.6 106.3 %collective-permute-start.40 = (bf16[4,256,1408]{2,1,0:T(8,128)(2,1)}, bf16[4,256,1408]{2,1,0:T(8,128)(2,1)}, u32[]{:S(2)}, u32[]{:S(2)}) collective-permute-start(bf16[4,256,1408]{2,1,0:T(8,128)(2,1)} %get-tuple-element.200.even_ref), channel_id=1, source_target_pairs={{0,4},{1,5},{2,6},{3,7},{4,0},{5,1},{6,2},{7,3}} | collective-permute-start | bytes 8650760 | tf_op jit(solution)/shard_map/ppermute | solution.py:159
  1132.2 101.6 %collective-permute-start.42 = (bf16[4,256,1408]{2,1,0:T(8,128)(2,1)}, bf16[4,256,1408]{2,1,0:T(8,128)(2,1)}, u32[]{:S(2)}, u32[]{:S(2)}) collective-permute-start(bf16[4,256,1408]{2,1,0:T(8,128)(2,1)} %get-tuple-element.200.even_ref), channel_id=1, source_target_pairs={{0,1},{1,0},{2,3},{3,2},{4,5},{5,4},{6,7},{7,6}} | collective-permute-start | bytes 8650760 | tf_op jit(solution)/shard_map/ppermute | solution.py:159
  (76 other events, 2389.9 us)

commit v3 on v2

--- a/solution.py
+++ b/solution.py
@@ -1,3 +1,4 @@
+import functools
 import math
 import jax
 import jax.numpy as jnp
@@ -7,6 +8,7 @@
 from jax.sharding import PartitionSpec as P
 
 NS_ITERS = 5
+SUM_ROWS = 32
 MOMENTUM = 0.95
 LEARN_RATE = 0.02
 WEIGHT_DECAY = 0.1
@@ -15,21 +17,24 @@
 COEF_B = -4.7750
 COEF_C = 2.0315
 
+CHUNKS = (((0, 4), (4, 4)),) * 3 + (((0, 3), (3, 3), (6, 1), (7, 1)),)
 AGENDA = (
     ("ns", 0, 0), ("ns", 0, 1), ("ns", 0, 2), ("ns", 0, 3), ("ns", 0, 4), ("out", 0),
     ("ns", 1, 0), ("ns", 1, 1), ("upd", 0), ("ns", 1, 2), ("ns", 1, 3), ("ns", 1, 4), ("out", 1),
-    ("ns", 2, 0), ("dg", 0), ("pp", 0, 1, 0), ("pp", 0, 2, 1), ("ns", 2, 1), ("ns", 2, 2), ("pp", 0, 1, 1), ("pp", 0, 2, 0), ("ns", 2, 3), ("ns", 2, 4),
+    ("ns", 2, 0), ("dg", 0, 0), ("pp", 0, 1, 0), ("pp", 0, 2, 1), ("ns", 2, 1), ("ns", 2, 2), ("pp", 0, 1, 1), ("pp", 0, 2, 0), ("ns", 2, 3), ("ns", 2, 4),
     ("upd", 1), ("out", 2), ("ns", 3, 0), ("ns", 3, 1), ("ns", 3, 2), ("pp", 0, 3, 0), ("pp", 0, 3, 1), ("ns", 3, 3), ("upd", 2), ("ns", 3, 4), ("out", 3),
     ("pl", 0, 0, 0), ("pl", 0, 0, 1), ("pl", 0, 1, 0), ("pl", 0, 1, 1), ("pl", 0, 2, 0), ("pl", 0, 2, 1), ("pl", 0, 3, 0), ("pl", 0, 3, 1),
-    ("dg", 1), ("pp", 1, 1, 0), ("pp", 1, 2, 1), ("pl", 1, 0, 0), ("pl", 1, 0, 1), ("pl", 1, 1, 0),
+    ("dg", 1, 0), ("pp", 1, 1, 0), ("pp", 1, 2, 1), ("pl", 1, 0, 0), ("pl", 1, 0, 1), ("pl", 1, 1, 0),
     ("pp", 1, 1, 1), ("pp", 1, 2, 0), ("pl", 1, 2, 1), ("pl", 1, 1, 1), ("pl", 1, 2, 0),
-    ("upd", 3), ("pl", 2, 0, 0), ("dg", 2), ("pp", 2, 1, 0), ("pp", 2, 2, 1), ("pl", 2, 0, 1), ("pl", 2, 1, 0),
+    ("upd", 3), ("pl", 2, 0, 0), ("dg", 2, 0), ("pp", 2, 1, 0), ("pp", 2, 2, 1), ("pl", 2, 0, 1), ("pl", 2, 1, 0),
     ("pp", 2, 1, 1), ("pp", 2, 2, 0), ("pl", 2, 2, 1), ("pl", 2, 1, 1), ("pl", 2, 2, 0),
-    ("pp", 1, 3, 0), ("pp", 1, 3, 1), ("pl", 3, 0, 0), ("pl", 1, 3, 0), ("pl", 1, 3, 1),
-    ("dg", 3), ("pp", 3, 1, 0), ("pp", 3, 2, 1), ("pl", 3, 0, 1), ("pl", 3, 1, 0),
-    ("pp", 3, 1, 1), ("pp", 3, 2, 0), ("pl", 3, 2, 1), ("pl", 3, 1, 1), ("pl", 3, 2, 0),
+    ("pp", 1, 3, 0), ("pp", 1, 3, 1), ("pl", 3, 0, 0), ("pl", 3, 0, 2), ("pl", 3, 0, 3), ("pl", 1, 3, 0), ("pl", 1, 3, 1),
+    ("dg", 3, 0), ("pp", 3, 1, 0), ("pp", 3, 2, 1), ("pl", 3, 0, 1),
+    ("dg", 3, 2), ("pp", 3, 1, 2), ("pp", 3, 2, 3), ("pl", 3, 1, 0), ("pl", 3, 2, 1), ("pl", 3, 1, 2), ("pl", 3, 2, 3),
+    ("pp", 3, 1, 1), ("pp", 3, 2, 0), ("pp", 3, 1, 3), ("pp", 3, 2, 2), ("pl", 3, 1, 1), ("pl", 3, 2, 0), ("pl", 3, 1, 3), ("pl", 3, 2, 2),
     ("pp", 2, 3, 0), ("pp", 2, 3, 1), ("pl", 2, 3, 0), ("pl", 2, 3, 1),
     ("pp", 3, 3, 0), ("pp", 3, 3, 1), ("pl", 3, 3, 0), ("pl", 3, 3, 1),
+    ("pp", 3, 3, 2), ("pp", 3, 3, 3), ("pl", 3, 3, 2), ("pl", 3, 3, 3),
 )
 
 
@@ -49,17 +54,31 @@
     return (COEF_A * x_mat.astype(jnp.float32) + prod_mat).astype(jnp.bfloat16)
 
 
-def momentum_body(me_ref, mom_ref, grad_ref, *refs):
-    new_ref, low_ref, sum_ref = refs[-3:]
-    new = MOMENTUM * mom_ref[...] + grad_ref[...].astype(jnp.float32)
-    new_ref[...] = new
-    low_ref[...] = new.astype(jnp.bfloat16)
-    sum_ref[...] = jnp.broadcast_to(jnp.sum(new * new), sum_ref.shape)
-
-
-def momentum_rows(me, mom_rows, grad_rows, whole, first, waves, group, by_distance):
+def momentum_body(outs, me_ref, mom_ref, grad_ref, *refs):
+    refs = dict(zip(outs, refs[-len(outs):]))
+    mats, rows, cols = mom_ref.shape
+    step = math.gcd(rows, SUM_ROWS)
+    for mat in range(mats):
+
+        def some_rows(i, total):
+            here = (mat, pl.ds(pl.multiple_of(i * step, step), step))
+            new = MOMENTUM * mom_ref[here] + grad_ref[here].astype(jnp.float32)
+            if "new" in refs:
+                refs["new"][here] = new
+            if "low" in refs:
+                refs["low"][here] = new.astype(jnp.bfloat16)
+                total = total + jnp.sum((new * new).reshape(step // 8, 8, cols), axis=0)
+            return total
+
+        total = lax.fori_loop(0, rows // step, some_rows, jnp.zeros((8, cols), jnp.float32))
+        if "sum" in refs:
+            refs["sum"][mat] = jnp.broadcast_to(jnp.sum(total), refs["sum"].shape[1:])
+
+
+def momentum_rows(me, mom_rows, grad_rows, outs, whole, first, waves, group, by_distance=False):
     total, rows, cols = mom_rows.shape
-    here = pl.BlockSpec((1, rows, cols), lambda k, d, me_ref: (first + k * group + d, 0, 0))
+    mats = 2 if waves == 1 and not by_distance else 1
+    here = pl.BlockSpec((mats, rows, cols), lambda k, d, me_ref: ((first + k * group) // mats + d, 0, 0))
     in_specs, operands, aliases = [here, here], [mom_rows, grad_rows], {}
     if whole is not None:
         in_specs.append(pl.BlockSpec(memory_space=pl.ANY))
@@ -70,23 +89,23 @@
         low_map = lambda k, d, me_ref: (lax.bitwise_xor(d, me_ref[0]), 0, 0)
     else:
         low_map = lambda k, d, me_ref: (d * waves + k, 0, 0)
+    specs = {
+        "new": (here, jax.ShapeDtypeStruct((total, rows, cols), jnp.float32)),
+        "low": (pl.BlockSpec((mats, rows, cols), low_map), jax.ShapeDtypeStruct((count, rows, cols), jnp.bfloat16)),
+        "sum": (
+            pl.BlockSpec((mats, 8, 128), lambda k, d, me_ref: (d * waves + k, 0, 0)),
+            jax.ShapeDtypeStruct((count, 8, 128), jnp.float32),
+        ),
+    }
     return pl.pallas_call(
-        momentum_body,
+        functools.partial(momentum_body, outs),
         grid_spec=pltpu.PrefetchScalarGridSpec(
             num_scalar_prefetch=1,
-            grid=(waves, group),
+            grid=(waves, group // mats),
             in_specs=in_specs,
-            out_specs=(
-                here,
-                pl.BlockSpec((1, rows, cols), low_map),
-                pl.BlockSpec((1, 8, 128), lambda k, d, me_ref: (d * waves + k, 0, 0)),
-            ),
+            out_specs=[specs[name][0] for name in outs],
         ),
-        out_shape=(
-            jax.ShapeDtypeStruct((total, rows, cols), jnp.float32),
-            jax.ShapeDtypeStruct((count, rows, cols), jnp.bfloat16),
-            jax.ShapeDtypeStruct((count, 8, 128), jnp.float32),
-        ),
+        out_shape=[specs[name][1] for name in outs],
         input_output_aliases=aliases,
         cost_estimate=pl.CostEstimate(flops=4 * count * rows * cols, bytes_accessed=12 * count * rows * cols, transcendentals=0),
     )(me, *operands)
@@ -160,9 +179,12 @@
 
         my_index = lax.axis_index("data")
         me = my_index.astype(jnp.int32).reshape(1)
-        mom_new, low_0, sum_0 = momentum_rows(me, mom_rows, grad_rows, None, 0, 1, group, False)
-        mom_new, low_1, sum_1 = momentum_rows(me, mom_rows, grad_rows, mom_new, group, 2, group, False)
-        mom_new, low_3, sum_3 = momentum_rows(me, mom_rows, grad_rows, mom_new, 3 * group, 1, group, True)
+        low_0, sum_0 = momentum_rows(me, mom_rows, grad_rows, ("low", "sum"), None, 0, 1, group)
+        mom_new, low_1, sum_1 = momentum_rows(me, mom_rows, grad_rows, ("new", "low", "sum"), None, group, 2, group)
+        mom_new, low_3, sum_3 = momentum_rows(
+            me, mom_rows, grad_rows, ("new", "low", "sum"), mom_new, 3 * group, 1, group, True
+        )
+        (mom_new,) = momentum_rows(me, mom_rows, grad_rows, ("new",), mom_new, 0, 1, group)
         part = jnp.concatenate([sum_0[:, 0, 0], sum_1[:, 0, 0], sum_3[:, 0, 0]])
         sq_total = part
         for bit in range(1, group):
@@ -180,18 +202,16 @@
             low = low_0 if wave == 0 else low_1[:, wave - 1]
             return (low.reshape(rows_all, col_count).astype(jnp.float32) / norm).astype(jnp.bfloat16)
 
-        half = group // 2
-
         def update(ortho, wave):
-            halves = []
-            for h in range(2):
-                w_old = lax.slice_in_dim(w_rows, wave * group + h * half, wave * group + (h + 1) * half)
-                part = lax.slice_in_dim(ortho, h * half, (h + 1) * half)
+            parts = []
+            for first, count in CHUNKS[wave]:
+                w_old = lax.slice_in_dim(w_rows, wave * group + first, wave * group + first + count)
+                part = lax.slice_in_dim(ortho, first, first + count)
                 w_new = w_old - LEARN_RATE * (part.astype(jnp.float32) * rms_scale + WEIGHT_DECAY * w_old)
-                halves.append(w_new.astype(jnp.bfloat16))
-            return lax.optimization_barrier(tuple(halves))
-
-        got = {(w, h): {} for w in range(waves) for h in range(2)}
+                parts.append(w_new.astype(jnp.bfloat16))
+            return parts
+
+        got = {(w, h): {} for w in range(waves) for h in range(len(CHUNKS[w]))}
         final = {}
         state = {"x": None, "params": None}
         outs = {}
@@ -217,9 +237,10 @@
                     mine[2] = hop(own, 2)
                     mine[4] = hop(own, 4)
             elif kind == "dg":
-                got[wave, 0][2], got[wave, 1][4] = tie(got[wave, 0][2], got[wave, 1][4])
-                got[wave, 0][6] = hop(got[wave, 0][2], 4)
-                got[wave, 1][6] = hop(got[wave, 1][4], 2)
+                even, odd = got[wave, where[0]], got[wave, where[0] + 1]
+                even[2], odd[4] = tie(even[2], odd[4])
+                even[6] = hop(even[2], 4)
+                odd[6] = hop(odd[4], 2)
             elif kind == "pp":
                 pair, h = where
                 mine = got[wave, h]
@@ -232,7 +253,7 @@
                 if state["params"] is None:
                     even = after(even, state["x"])
                 state["params"] = place(
-                    state["params"], me, even, mine[2 * pair + 1], pair, wave * group + h * half, mat_count, group
+                    state["params"], me, even, mine[2 * pair + 1], pair, wave * group + CHUNKS[wave][h][0], mat_count, group
                 )
             if kind == "ns" and where[0] == NS_ITERS - 1:
                 final[wave] = state["x"]

time: 1660 us -> 1700 us (1.024)
  Pallas kernels: 242 us -> 264 us
    pallas_call x32 -> x40, Pallas kernels: 179 us -> 196 us  [place(): pl.pallas_call(place_body, grid_spec=pltpu.PrefetchScalarGridSpec(num_sca...]
    ppermute x70 -> x84, waiting for transfers between devices: 575 us -> 588 us  [hop(): return lax.ppermute(array, 'data', [(i, i ^ bit) for i in range(group)])]
    ppermute x70 -> x84, starting transfers between devices: 59 us -> 66.5 us  [hop(): return lax.ppermute(array, 'data', [(i, i ^ bit) for i in range(group)])]
    pallas_call x3 -> x4, Pallas kernels: 57.6 us -> 62.3 us  [momentum_rows(): pl.pallas_call(functools.partial(momentum_body, outs), grid_spec=pltpu.Pr...]
    convert_element_type x4 -> x5, other arithmetic: 37.9 us -> 39.5 us  [update(): parts.append(w_new.astype(jnp.bfloat16))]
  transfers between devices with their start and end apart: 76 -> 90, of which waited for: 27 -> 33; matrix products, arithmetic and copies ran while one was open for 38% -> 37% of each run, Pallas kernels for 14% -> 15%
where the time goes in v3:
time: 1700 us; the launch traced here: 1690 us
  waiting for transfers between devices  685 us (40%)
  matrix products  569 us (33%)
  Pallas kernels  264 us (16%)
  starting transfers between devices  89.7 us (5%)
  other arithmetic  51.7 us (3%)
  local copies, waits for them, and re-layouts  23.4 us (1%)
    ppermute x84, waiting for transfers between devices, hop(): return lax.ppermute(array, 'data', [(i, i ^ bit) for i in range(group)])  588 us
    dot_general x20, matrix products, ns_step(): jnp.einsum(eq, poly_mat, x_mat, preferred_element_type=jnp.float32)  219 us
    dot_general x20, matrix products, ns_step(): jnp.einsum(eq, x_mat, x_mat, preferred_element_type=jnp.float32)  209 us
    pallas_call x40, Pallas kernels, place(): pl.pallas_call(place_body, grid_spec=pltpu.PrefetchScalarGridSpec(num_sca...  196 us
    dot_general x20, matrix products, ns_step(): square = jnp.dot(gram_mat, gram_mat, preferred_element_type=jnp.float32)  141 us
    all_to_all x6, waiting for transfers between devices, exchange(): return lax.all_to_all(array, 'data', 0, 0, tiled=True)  97.4 us
    ppermute x84, starting transfers between devices, hop(): return lax.ppermute(array, 'data', [(i, i ^ bit) for i in range(group)])  66.5 us
    pallas_call x4, Pallas kernels, momentum_rows(): pl.pallas_call(functools.partial(momentum_body, outs), grid_spec=pltpu.Pr...  62.3 us
  transfers between devices with their start and end apart: 90, of which 33 were waited for; matrix products, arithmetic and copies ran while one was open for 37% of the time, Pallas kernels for 15%

profile of v3, /device:TPU:0, one launch (start us, length us, event | category | flops | bytes accessed | tf_op | source)
XLA Modules:
  0.0 1687.6 jit_solution(3016196708317213223)
XLA Ops:
  14.4 28.3 %shard_map.51 = (f32[32,256,1408]{2,1,0:T(8,128)}, bf16[16,256,1408]{2,1,0:T(8,128)(2,1)}, f32[16,8,128]{2,1,0:T(8,128)}) custom-call(s32[1]{0:T(128)} %bitcast.me_ref, f32[32,256,1408]{2,1,0:T(8,128)} %mom_ref.7, bf16[32,256,1408]{2,1,0:T(8,128)(2,1)} %grad_ref.7), custom_call_target="tpu_custom_call" | custom-call | flops 23068672 | bytes 69206016 | tf_op jit(solution)/shard_map/pallas_call | solution.py:100
  42.7 14.4 shard_map.52
  178.1 13.2 convolution_convert_fusion.16
  237.2 68.6 %all-to-all-done.1 = bf16[16,256,1408]{2,1,0:T(8,128)(2,1)} async-done(((bf16[16,256,1408]{2,1,0:T(8,128)(2,1)}), bf16[16,256,1408]{2,1,0:T(8,128)(2,1)}, u32[]{:S(2)}, u32[]{:S(2)}) %all-to-all-start.1) | async-done | bytes 11534368 | tf_op jit(solution)/shard_map/all_to_all | solution.py:175
  457.7 14.0 add_convert_fusion.10
  505.9 41.5 %collective-permute-done.14.even_ref = bf16[4,256,1408]{2,1,0:T(8,128)(2,1)} collective-permute-done((bf16[4,256,1408]{2,1,0:T(8,128)(2,1)}, bf16[4,256,1408]{2,1,0:T(8,128)(2,1)}, u32[]{:S(2)}, u32[]{:S(2)}) %collective-permute-start.14) | collective-permute-done | bytes 2883616 | tf_op jit(solution)/shard_map/ppermute | solution.py:178
  548.9 13.7 convolution_convert_fusion.8
  606.7 62.2 %collective-permute-done.16.even_ref = bf16[4,256,1408]{2,1,0:T(8,128)(2,1)} collective-permute-done((bf16[4,256,1408]{2,1,0:T(8,128)(2,1)}, bf16[4,256,1408]{2,1,0:T(8,128)(2,1)}, u32[]{:S(2)}, u32[]{:S(2)}) %collective-permute-start.16) | collective-permute-done | bytes 2883616 | tf_op jit(solution)/shard_map/ppermute | solution.py:178
  744.6 67.3 %collective-permute-done.8.refs_2_ = bf16[1,256,1408]{2,1,0:T(8,128)(2,1)S(1)} collective-permute-done((bf16[1,256,1408]{2,1,0:T(8,128)(2,1)}, bf16[1,256,1408]{2,1,0:T(8,128)(2,1)S(1)}, u32[]{:S(2)}, u32[]{:S(2)}) %collective-permute-start.8) | collective-permute-done | bytes 720928 | tf_op jit(solution)/shard_map/ppermute | solution.py:178
  812.8 13.5 collective-permute-done.9.refs_3_
  834.6 13.7 convolution_convert_fusion.4
  980.7 12.0 add_convert_fusion
  1060.6 43.0 %collective-permute-done.33.even_ref = bf16[4,256,1408]{2,1,0:T(8,128)(2,1)} collective-permute-done((bf16[4,256,1408]{2,1,0:T(8,128)(2,1)}, bf16[4,256,1408]{2,1,0:T(8,128)(2,1)}, u32[]{:S(2)}, u32[]{:S(2)}) %collective-permute-start.33) | collective-permute-done | bytes 2883616 | tf_op jit(solution)/shard_map/ppermute | solution.py:178
  1105.6 16.0 collective-permute-start.40
  1140.0 26.9 %all-to-all-done.5 = bf16[8,256,1408]{2,1,0:T(8,128)(2,1)} async-done(((bf16[8,256,1408]{2,1,0:T(8,128)(2,1)}), bf16[8,256,1408]{2,1,0:T(8,128)(2,1)}, u32[]{:S(2)}, u32[]{:S(2)}) %all-to-all-start.5) | async-done | bytes 5767200 | tf_op jit(solution)/shard_map/all_to_all | solution.py:175
  1183.4 43.3 %collective-permute-done.40.even_ref = bf16[4,256,1408]{2,1,0:T(8,128)(2,1)} collective-permute-done((bf16[4,256,1408]{2,1,0:T(8,128)(2,1)}, bf16[4,256,1408]{2,1,0:T(8,128)(2,1)}, u32[]{:S(2)}, u32[]{:S(2)}) %collective-permute-start.40) | collective-permute-done | bytes 2883616 | tf_op jit(solution)/shard_map/ppermute | solution.py:178
  1241.5 51.5 %collective-permute-done.44.even_ref = bf16[4,256,1408]{2,1,0:T(8,128)(2,1)} collective-permute-done((bf16[4,256,1408]{2,1,0:T(8,128)(2,1)}, bf16[4,256,1408]{2,1,0:T(8,128)(2,1)}, u32[]{:S(2)}, u32[]{:S(2)}) %collective-permute-start.44) | collective-permute-done | bytes 2883616 | tf_op jit(solution)/shard_map/ppermute | solution.py:178
  1313.9 44.6 %collective-permute-done.49.even_ref = bf16[4,256,1408]{2,1,0:T(8,128)(2,1)} collective-permute-done((bf16[4,256,1408]{2,1,0:T(8,128)(2,1)}, bf16[4,256,1408]{2,1,0:T(8,128)(2,1)}, u32[]{:S(2)}, u32[]{:S(2)}) %collective-permute-start.49) | collective-permute-done | bytes 2883616 | tf_op jit(solution)/shard_map/ppermute | solution.py:178
  1395.1 23.5 %collective-permute-done.56.even_ref = bf16[3,256,1408]{2,1,0:T(8,128)(2,1)} collective-permute-done((bf16[3,256,1408]{2,1,0:T(8,128)(2,1)}, bf16[3,256,1408]{2,1,0:T(8,128)(2,1)}, u32[]{:S(2)}, u32[]{:S(2)}) %collective-permute-start.56) | collective-permute-done | bytes 2162720 | tf_op jit(solution)/shard_map/ppermute | solution.py:178
  1422.9 16.9 collective-permute-done.58.even_ref
  1487.5 17.8 %collective-permute-done.65.even_ref = bf16[3,256,1408]{2,1,0:T(8,128)(2,1)} collective-permute-done((bf16[3,256,1408]{2,1,0:T(8,128)(2,1)}, bf16[3,256,1408]{2,1,0:T(8,128)(2,1)}, u32[]{:S(2)}, u32[]{:S(2)}) %collective-permute-start.65) | collective-permute-done | bytes 2162720 | tf_op jit(solution)/shard_map/ppermute | solution.py:178
  1506.6 60.0 %collective-permute-done.66.even_ref = bf16[1,256,1408]{2,1,0:T(8,128)(2,1)} collective-permute-done((bf16[1,256,1408]{2,1,0:T(8,128)(2,1)S(1)}, bf16[1,256,1408]{2,1,0:T(8,128)(2,1)}, u32[]{:S(2)}, u32[]{:S(2)}) %collective-permute-start.66) | collective-permute-done | bytes 720928 | tf_op jit(solution)/shard_map/ppermute | solution.py:178
  1568.1 16.0 collective-permute-done.67.even_ref
  1618.3 31.5 %collective-permute-done.76.even_ref = bf16[3,256,1408]{2,1,0:T(8,128)(2,1)} collective-permute-done((bf16[3,256,1408]{2,1,0:T(8,128)(2,1)}, bf16[3,256,1408]{2,1,0:T(8,128)(2,1)}, u32[]{:S(2)}, u32[]{:S(2)}) %collective-permute-start.76) | collective-permute-done | bytes 2162720 | tf_op jit(solution)/shard_map/ppermute | solution.py:178
  (341 shorter events, 929.6 us)
Async XLA Ops:
  80.1 650.9 %collective-permute-start.10 = (bf16[1,256,1408]{2,1,0:T(8,128)(2,1)}, bf16[1,256,1408]{2,1,0:T(8,128)(2,1)}, u32[]{:S(2)}, u32[]{:S(2)}) collective-permute-start(bf16[1,256,1408]{2,1,0:T(8,128)(2,1)} %get-tuple-element.137), channel_id=1, source_target_pairs={{0,4},{1,5},{2,6},{3,7},{4,0},{5,1},{6,2},{7,3}} | collective-permute-start | bytes 2162696 | tf_op jit(solution)/shard_map/ppermute | solution.py:178
  81.1 651.9 %collective-permute-start.11 = (bf16[1,256,1408]{2,1,0:T(8,128)(2,1)}, bf16[1,256,1408]{2,1,0:T(8,128)(2,1)}, u32[]{:S(2)}, u32[]{:S(2)}) collective-permute-start(bf16[1,256,1408]{2,1,0:T(8,128)(2,1)} %get-tuple-element.138), channel_id=1, source_target_pairs={{0,5},{1,4},{2,7},{3,6},{4,1},{5,0},{6,3},{7,2}} | collective-permute-start | bytes 2162696 | tf_op jit(solution)/shard_map/ppermute | solution.py:178
  82.7 659.7 %collective-permute-start.12 = (bf16[1,256,1408]{2,1,0:T(8,128)(2,1)}, bf16[1,256,1408]{2,1,0:T(8,128)(2,1)}, u32[]{:S(2)}, u32[]{:S(2)}) collective-permute-start(bf16[1,256,1408]{2,1,0:T(8,128)(2,1)} %get-tuple-element.139), channel_id=1, source_target_pairs={{0,6},{1,7},{2,4},{3,5},{4,2},{5,3},{6,0},{7,1}} | collective-permute-start | bytes 2162696 | tf_op jit(solution)/shard_map/ppermute | solution.py:178
  173.9 131.9 %all-to-all-start.1 = ((bf16[16,256,1408]{2,1,0:T(8,128)(2,1)}), bf16[16,256,1408]{2,1,0:T(8,128)(2,1)}, u32[]{:S(2)}, u32[]{:S(2)}) async-start(bf16[16,256,1408]{2,1,0:T(8,128)(2,1)} %get-tuple-element.143), calls=%async_computation.1 | async-start | bytes 23068672 | tf_op jit(solution)/shard_map/all_to_all | solution.py:175
  502.0 225.4 %all-to-all-start.3 = ((bf16[8,256,1408]{2,1,0:T(8,128)(2,1)}), bf16[8,256,1408]{2,1,0:T(8,128)(2,1)}, u32[]{:S(2)}, u32[]{:S(2)}) async-start(bf16[8,256,1408]{2,1,0:T(8,128)(2,1)} %bitcast.146), calls=%async_computation.3 | async-start | bytes 11534336 | tf_op jit(solution)/shard_map/all_to_all | solution.py:175
  547.4 121.5 %collective-permute-start.16 = (bf16[4,256,1408]{2,1,0:T(8,128)(2,1)}, bf16[4,256,1408]{2,1,0:T(8,128)(2,1)}, u32[]{:S(2)}, u32[]{:S(2)}) collective-permute-start(bf16[4,256,1408]{2,1,0:T(8,128)(2,1)} %get-tuple-element.150.even_ref), channel_id=1, source_target_pairs={{0,2},{1,3},{2,0},{3,1},{4,6},{5,7},{6,4},{7,5}} | collective-permute-start | bytes 8650760 | tf_op jit(solution)/shard_map/ppermute | solution.py:178
  547.9 122.4 %collective-permute-start.17 = (bf16[4,256,1408]{2,1,0:T(8,128)(2,1)}, bf16[4,256,1408]{2,1,0:T(8,128)(2,1)}, u32[]{:S(2)}, u32[]{:S(2)}) collective-permute-start(bf16[4,256,1408]{2,1,0:T(8,128)(2,1)} %get-tuple-element.181.even_ref), channel_id=1, source_target_pairs={{0,4},{1,5},{2,6},{3,7},{4,0},{5,1},{6,2},{7,3}} | collective-permute-start | bytes 8650760 | tf_op jit(solution)/shard_map/ppermute | solution.py:178
  727.4 221.7 %all-to-all-start.4 = ((bf16[8,256,1408]{2,1,0:T(8,128)(2,1)}), bf16[8,256,1408]{2,1,0:T(8,128)(2,1)}, u32[]{:S(2)}, u32[]{:S(2)}) async-start(bf16[8,256,1408]{2,1,0:T(8,128)(2,1)} %bitcast.145), calls=%async_computation.4 | async-start | bytes 11534336 | tf_op jit(solution)/shard_map/all_to_all | solution.py:175
  731.0 80.9 %collective-permute-start.8 = (bf16[1,256,1408]{2,1,0:T(8,128)(2,1)}, bf16[1,256,1408]{2,1,0:T(8,128)(2,1)S(1)}, u32[]{:S(2)}, u32[]{:S(2)}) collective-permute-start(bf16[1,256,1408]{2,1,0:T(8,128)(2,1)} %get-tuple-element.135), channel_id=1, source_target_pairs={{0,2},{1,3},{2,0},{3,1},{4,6},{5,7},{6,4},{7,5}} | collective-permute-start | bytes 2162696 | tf_op jit(solution)/shard_map/ppermute | solution.py:178
  733.0 93.3 %collective-permute-start.9 = (bf16[1,256,1408]{2,1,0:T(8,128)(2,1)}, bf16[1,256,1408]{2,1,0:T(8,128)(2,1)S(1)}, u32[]{:S(2)}, u32[]{:S(2)}) collective-permute-start(bf16[1,256,1408]{2,1,0:T(8,128)(2,1)} %get-tuple-element.136), channel_id=1, source_target_pairs={{0,3},{1,2},{2,1},{3,0},{4,7},{5,6},{6,5},{7,4}} | collective-permute-start | bytes 2162696 | tf_op jit(solution)/shard_map/ppermute | solution.py:178
  742.4 216.2 %collective-permute-start.27 = (bf16[4,256,1408]{2,1,0:T(8,128)(2,1)}, bf16[4,256,1408]{2,1,0:T(8,128)(2,1)}, u32[]{:S(2)}, u32[]{:S(2)}) collective-permute-start(bf16[4,256,1408]{2,1,0:T(8,128)(2,1)} %get-tuple-element.181.even_ref), channel_id=1, source_target_pairs={{0,1},{1,0},{2,3},{3,2},{4,5},{5,4},{6,7},{7,6}} | collective-permute-start | bytes 8650760 | tf_op jit(solution)/shard_map/ppermute | solution.py:178
  742.6 226.9 %collective-permute-start.26 = (bf16[4,256,1408]{2,1,0:T(8,128)(2,1)}, bf16[4,256,1408]{2,1,0:T(8,128)(2,1)}, u32[]{:S(2)}, u32[]{:S(2)}) collective-permute-start(bf16[4,256,1408]{2,1,0:T(8,128)(2,1)} %get-tuple-element.150.even_ref), channel_id=1, source_target_pairs={{0,1},{1,0},{2,3},{3,2},{4,5},{5,4},{6,7},{7,6}} | collective-permute-start | bytes 8650760 | tf_op jit(solution)/shard_map/ppermute | solution.py:178
  742.9 176.9 %collective-permute-start.18 = (bf16[4,256,1408]{2,1,0:T(8,128)(2,1)}, bf16[4,256,1408]{2,1,0:T(8,128)(2,1)}, u32[]{:S(2)}, u32[]{:S(2)}) collective-permute-start(bf16[4,256,1408]{2,1,0:T(8,128)(2,1)} %collective-permute-done.14.even_ref), channel_id=1, source_target_pairs={{0,4},{1,5},{2,6},{3,7},{4,0},{5,1},{6,2},{7,3}} | collective-permute-start | bytes 8650760 | tf_op jit(solution)/shard_map/ppermute | solution.py:178
  812.0 107.9 %collective-permute-start.19 = (bf16[4,256,1408]{2,1,0:T(8,128)(2,1)S(1)}, bf16[4,256,1408]{2,1,0:T(8,128)(2,1)}, u32[]{:S(2)}, u32[]{:S(2)}) collective-permute-start(bf16[4,256,1408]{2,1,0:T(8,128)(2,1)S(1)} %copy-done.7), channel_id=1, source_target_pairs={{0,2},{1,3},{2,0},{3,1},{4,6},{5,7},{6,4},{7,5}} | collective-permute-start | bytes 8650760 | tf_op jit(solution)/shard_map/ppermute | solution.py:178
  827.2 142.4 %collective-permute-start.25 = (bf16[4,256,1408]{2,1,0:T(8,128)(2,1)}, bf16[4,256,1408]{2,1,0:T(8,128)(2,1)}, u32[]{:S(2)}, u32[]{:S(2)}) collective-permute-start(bf16[4,256,1408]{2,1,0:T(8,128)(2,1)} %collective-permute-done.14.even_ref), channel_id=1, source_target_pairs={{0,1},{1,0},{2,3},{3,2},{4,5},{5,4},{6,7},{7,6}} | collective-permute-start | bytes 8650760 | tf_op jit(solution)/shard_map/ppermute | solution.py:178
  1039.9 127.0 %all-to-all-start.5 = ((bf16[8,256,1408]{2,1,0:T(8,128)(2,1)}), bf16[8,256,1408]{2,1,0:T(8,128)(2,1)}, u32[]{:S(2)}, u32[]{:S(2)}) async-start(bf16[8,256,1408]{2,1,0:T(8,128)(2,1)} %bitcast.144), calls=%async_computation.5 | async-start | bytes 11534336 | tf_op jit(solution)/shard_map/all_to_all | solution.py:175
  1043.4 78.1 %collective-permute-start.37 = (bf16[4,256,1408]{2,1,0:T(8,128)(2,1)}, bf16[4,256,1408]{2,1,0:T(8,128)(2,1)}, u32[]{:S(2)}, u32[]{:S(2)}) collective-permute-start(bf16[4,256,1408]{2,1,0:T(8,128)(2,1)} %collective-permute-done.29.even_ref), channel_id=1, source_target_pairs={{0,1},{1,0},{2,3},{3,2},{4,5},{5,4},{6,7},{7,6}} | collective-permute-start | bytes 8650760 | tf_op jit(solution)/shard_map/ppermute | solution.py:178
  1105.6 121.2 %collective-permute-start.40 = (bf16[4,256,1408]{2,1,0:T(8,128)(2,1)}, bf16[4,256,1408]{2,1,0:T(8,128)(2,1)}, u32[]{:S(2)}, u32[]{:S(2)}) collective-permute-start(bf16[4,256,1408]{2,1,0:T(8,128)(2,1)} %get-tuple-element.198.even_ref), channel_id=1, source_target_pairs={{0,2},{1,3},{2,0},{3,1},{4,6},{5,7},{6,4},{7,5}} | collective-permute-start | bytes 8650760 | tf_op jit(solution)/shard_map/ppermute | solution.py:178
  1121.6 106.3 %collective-permute-start.41 = (bf16[4,256,1408]{2,1,0:T(8,128)(2,1)}, bf16[4,256,1408]{2,1,0:T(8,128)(2,1)}, u32[]{:S(2)}, u32[]{:S(2)}) collective-permute-start(bf16[4,256,1408]{2,1,0:T(8,128)(2,1)} %get-tuple-element.200.even_ref), channel_id=1, source_target_pairs={{0,4},{1,5},{2,6},{3,7},{4,0},{5,1},{6,2},{7,3}} | collective-permute-start | bytes 8650760 | tf_op jit(solution)/shard_map/ppermute | solution.py:178
  1127.2 101.6 %collective-permute-start.43 = (bf16[4,256,1408]{2,1,0:T(8,128)(2,1)}, bf16[4,256,1408]{2,1,0:T(8,128)(2,1)}, u32[]{:S(2)}, u32[]{:S(2)}) collective-permute-start(bf16[4,256,1408]{2,1,0:T(8,128)(2,1)} %get-tuple-element.200.even_ref), channel_id=1, source_target_pairs={{0,1},{1,0},{2,3},{3,2},{4,5},{5,4},{6,7},{7,6}} | collective-permute-start | bytes 8650760 | tf_op jit(solution)/shard_map/ppermute | solution.py:178
  1485.7 98.4 %collective-permute-start.71 = (bf16[3,256,1408]{2,1,0:T(8,128)(2,1)}, bf16[3,256,1408]{2,1,0:T(8,128)(2,1)}, u32[]{:S(2)}, u32[]{:S(2)}) collective-permute-start(bf16[3,256,1408]{2,1,0:T(8,128)(2,1)} %collective-permute-done.64.even_ref), channel_id=1, source_target_pairs={{0,1},{1,0},{2,3},{3,2},{4,5},{5,4},{6,7},{7,6}} | collective-permute-start | bytes 6488072 | tf_op jit(solution)/shard_map/ppermute | solution.py:178
  1485.7 114.2 %collective-permute-start.72 = (bf16[4,256,1408]{2,1,0:T(8,128)(2,1)}, bf16[4,256,1408]{2,1,0:T(8,128)(2,1)}, u32[]{:S(2)}, u32[]{:S(2)}) collective-permute-start(bf16[4,256,1408]{2,1,0:T(8,128)(2,1)} %collective-permute-done.40.even_ref), channel_id=1, source_target_pairs={{0,4},{1,5},{2,6},{3,7},{4,0},{5,1},{6,2},{7,3}} | collective-permute-start | bytes 8650760 | tf_op jit(solution)/shard_map/ppermute | solution.py:178
  1486.2 113.7 %collective-permute-start.73 = (bf16[4,256,1408]{2,1,0:T(8,128)(2,1)}, bf16[4,256,1408]{2,1,0:T(8,128)(2,1)}, u32[]{:S(2)}, u32[]{:S(2)}) collective-permute-start(bf16[4,256,1408]{2,1,0:T(8,128)(2,1)} %collective-permute-done.41.even_ref), channel_id=1, source_target_pairs={{0,2},{1,3},{2,0},{3,1},{4,6},{5,7},{6,4},{7,5}} | collective-permute-start | bytes 8650760 | tf_op jit(solution)/shard_map/ppermute | solution.py:178
  1505.3 84.5 %collective-permute-start.70 = (bf16[3,256,1408]{2,1,0:T(8,128)(2,1)}, bf16[3,256,1408]{2,1,0:T(8,128)(2,1)}, u32[]{:S(2)}, u32[]{:S(2)}) collective-permute-start(bf16[3,256,1408]{2,1,0:T(8,128)(2,1)} %collective-permute-done.65.even_ref), channel_id=1, source_target_pairs={{0,1},{1,0},{2,3},{3,2},{4,5},{5,4},{6,7},{7,6}} | collective-permute-start | bytes 6488072 | tf_op jit(solution)/shard_map/ppermute | solution.py:178
  (97 other events, 3020.1 us)

commit v4 on v3

--- a/solution.py
+++ b/solution.py
@@ -57,7 +57,7 @@
 def momentum_body(outs, me_ref, mom_ref, grad_ref, *refs):
     refs = dict(zip(outs, refs[-len(outs):]))
     mats, rows, cols = mom_ref.shape
-    step = math.gcd(rows, SUM_ROWS)
+    step = math.gcd(rows, SUM_ROWS) if mats > 1 else rows
     for mat in range(mats):
 
         def some_rows(i, total):
@@ -134,13 +134,13 @@
     out_ref = refs[-1]
     rows = even_ref.shape[1]
     swap = lax.rem(me_ref[0], 2)
-    out_ref[0, pl.ds(pl.multiple_of(swap * rows, rows), rows)] = even_ref[0]
-    out_ref[0, pl.ds(pl.multiple_of((1 - swap) * rows, rows), rows)] = odd_ref[0]
+    out_ref[:, pl.ds(pl.multiple_of(swap * rows, rows), rows)] = even_ref[...]
+    out_ref[:, pl.ds(pl.multiple_of((1 - swap) * rows, rows), rows)] = odd_ref[...]
 
 
 def place(whole, me, even, odd, pair, first, total, group):
     mats, rows, cols = even.shape
-    piece = pl.BlockSpec((1, rows, cols), lambda i, me_ref: (i, 0, 0))
+    piece = pl.BlockSpec((mats, rows, cols), lambda i, me_ref: (i, 0, 0))
     in_specs, operands, aliases = [piece, piece], [even, odd], {}
     if whole is not None:
         in_specs.append(pl.BlockSpec(memory_space=pl.ANY))
@@ -150,9 +150,9 @@
         place_body,
         grid_spec=pltpu.PrefetchScalarGridSpec(
             num_scalar_prefetch=1,
-            grid=(mats,),
+            grid=(1,),
             in_specs=in_specs,
-            out_specs=pl.BlockSpec((1, 2 * rows, cols), lambda i, me_ref: (i + first, lax.bitwise_xor(me_ref[0] // 2, pair), 0)),
+            out_specs=pl.BlockSpec((mats, 2 * rows, cols), lambda i, me_ref: (first // mats, lax.bitwise_xor(me_ref[0] // 2, pair), 0)),
         ),
         out_shape=jax.ShapeDtypeStruct((total, rows * group, cols), even.dtype),
         input_output_aliases=aliases,

time: 1700 us -> 1700 us (level)
  no operation moved by 1% of the time
where the time goes in v4:
time: 1700 us; the launch traced here: 1690 us
  waiting for transfers between devices  687 us (40%)
  matrix products  569 us (33%)
  Pallas kernels  261 us (15%)
  starting transfers between devices  89.4 us (5%)
  other arithmetic  51.9 us (3%)
  local copies, waits for them, and re-layouts  23.4 us (1%)
    ppermute x84, waiting for transfers between devices, hop(): return lax.ppermute(array, 'data', [(i, i ^ bit) for i in range(group)])  590 us
    dot_general x20, matrix products, ns_step(): jnp.einsum(eq, poly_mat, x_mat, preferred_element_type=jnp.float32)  219 us
    dot_general x20, matrix products, ns_step(): jnp.einsum(eq, x_mat, x_mat, preferred_element_type=jnp.float32)  209 us
    pallas_call x40, Pallas kernels, place(): pl.pallas_call(place_body, grid_spec=pltpu.PrefetchScalarGridSpec(num_sca...  193 us
    dot_general x20, matrix products, ns_step(): square = jnp.dot(gram_mat, gram_mat, preferred_element_type=jnp.float32)  141 us
    all_to_all x6, waiting for transfers between devices, exchange(): return lax.all_to_all(array, 'data', 0, 0, tiled=True)  97.1 us
    ppermute x84, starting transfers between devices, hop(): return lax.ppermute(array, 'data', [(i, i ^ bit) for i in range(group)])  66.6 us
    pallas_call x4, Pallas kernels, momentum_rows(): pl.pallas_call(functools.partial(momentum_body, outs), grid_spec=pltpu.Pr...  62.6 us
  transfers between devices with their start and end apart: 90, of which 33 were waited for; matrix products, arithmetic and copies ran while one was open for 37% of the time, Pallas kernels for 15%

profile of v4, /device:TPU:0, one launch (start us, length us, event | category | flops | bytes accessed | tf_op | source)
XLA Modules:
  0.0 1687.0 jit_solution(15296297980355601880)
XLA Ops:
  14.4 28.5 %shard_map.51 = (f32[32,256,1408]{2,1,0:T(8,128)}, bf16[16,256,1408]{2,1,0:T(8,128)(2,1)}, f32[16,8,128]{2,1,0:T(8,128)}) custom-call(s32[1]{0:T(128)} %bitcast.me_ref, f32[32,256,1408]{2,1,0:T(8,128)} %mom_ref.7, bf16[32,256,1408]{2,1,0:T(8,128)(2,1)} %grad_ref.7), custom_call_target="tpu_custom_call" | custom-call | flops 23068672 | bytes 69206016 | tf_op jit(solution)/shard_map/pallas_call | solution.py:100
  42.9 14.5 shard_map.52
  178.1 13.2 convolution_convert_fusion.16
  237.5 68.4 %all-to-all-done.1 = bf16[16,256,1408]{2,1,0:T(8,128)(2,1)} async-done(((bf16[16,256,1408]{2,1,0:T(8,128)(2,1)}), bf16[16,256,1408]{2,1,0:T(8,128)(2,1)}, u32[]{:S(2)}, u32[]{:S(2)}) %all-to-all-start.1) | async-done | bytes 11534368 | tf_op jit(solution)/shard_map/all_to_all | solution.py:175
  457.5 14.0 add_convert_fusion.10
  505.7 41.7 %collective-permute-done.14.even_ref = bf16[4,256,1408]{2,1,0:T(8,128)(2,1)} collective-permute-done((bf16[4,256,1408]{2,1,0:T(8,128)(2,1)}, bf16[4,256,1408]{2,1,0:T(8,128)(2,1)}, u32[]{:S(2)}, u32[]{:S(2)}) %collective-permute-start.14) | collective-permute-done | bytes 2883616 | tf_op jit(solution)/shard_map/ppermute | solution.py:178
  549.0 13.7 convolution_convert_fusion.8
  606.8 62.1 %collective-permute-done.16.even_ref = bf16[4,256,1408]{2,1,0:T(8,128)(2,1)} collective-permute-done((bf16[4,256,1408]{2,1,0:T(8,128)(2,1)}, bf16[4,256,1408]{2,1,0:T(8,128)(2,1)}, u32[]{:S(2)}, u32[]{:S(2)}) %collective-permute-start.16) | collective-permute-done | bytes 2883616 | tf_op jit(solution)/shard_map/ppermute | solution.py:178
  744.7 67.3 %collective-permute-done.8.refs_2_ = bf16[1,256,1408]{2,1,0:T(8,128)(2,1)S(1)} collective-permute-done((bf16[1,256,1408]{2,1,0:T(8,128)(2,1)}, bf16[1,256,1408]{2,1,0:T(8,128)(2,1)S(1)}, u32[]{:S(2)}, u32[]{:S(2)}) %collective-permute-start.8) | collective-permute-done | bytes 720928 | tf_op jit(solution)/shard_map/ppermute | solution.py:178
  812.9 13.5 collective-permute-done.9.refs_3_
  834.6 13.7 convolution_convert_fusion.4
  1061.2 42.9 %collective-permute-done.33.even_ref = bf16[4,256,1408]{2,1,0:T(8,128)(2,1)} collective-permute-done((bf16[4,256,1408]{2,1,0:T(8,128)(2,1)}, bf16[4,256,1408]{2,1,0:T(8,128)(2,1)}, u32[]{:S(2)}, u32[]{:S(2)}) %collective-permute-start.33) | collective-permute-done | bytes 2883616 | tf_op jit(solution)/shard_map/ppermute | solution.py:178
  1106.1 16.0 collective-permute-start.40
  1140.6 26.8 %all-to-all-done.5 = bf16[8,256,1408]{2,1,0:T(8,128)(2,1)} async-done(((bf16[8,256,1408]{2,1,0:T(8,128)(2,1)}), bf16[8,256,1408]{2,1,0:T(8,128)(2,1)}, u32[]{:S(2)}, u32[]{:S(2)}) %all-to-all-start.5) | async-done | bytes 5767200 | tf_op jit(solution)/shard_map/all_to_all | solution.py:175
  1184.2 43.1 %collective-permute-done.40.even_ref = bf16[4,256,1408]{2,1,0:T(8,128)(2,1)} collective-permute-done((bf16[4,256,1408]{2,1,0:T(8,128)(2,1)}, bf16[4,256,1408]{2,1,0:T(8,128)(2,1)}, u32[]{:S(2)}, u32[]{:S(2)}) %collective-permute-start.40) | collective-permute-done | bytes 2883616 | tf_op jit(solution)/shard_map/ppermute | solution.py:178
  1242.2 51.4 %collective-permute-done.44.even_ref = bf16[4,256,1408]{2,1,0:T(8,128)(2,1)} collective-permute-done((bf16[4,256,1408]{2,1,0:T(8,128)(2,1)}, bf16[4,256,1408]{2,1,0:T(8,128)(2,1)}, u32[]{:S(2)}, u32[]{:S(2)}) %collective-permute-start.44) | collective-permute-done | bytes 2883616 | tf_op jit(solution)/shard_map/ppermute | solution.py:178
  1314.6 44.5 %collective-permute-done.49.even_ref = bf16[4,256,1408]{2,1,0:T(8,128)(2,1)} collective-permute-done((bf16[4,256,1408]{2,1,0:T(8,128)(2,1)}, bf16[4,256,1408]{2,1,0:T(8,128)(2,1)}, u32[]{:S(2)}, u32[]{:S(2)}) %collective-permute-start.49) | collective-permute-done | bytes 2883616 | tf_op jit(solution)/shard_map/ppermute | solution.py:178
  1395.2 23.9 %collective-permute-done.56.even_ref = bf16[3,256,1408]{2,1,0:T(8,128)(2,1)} collective-permute-done((bf16[3,256,1408]{2,1,0:T(8,128)(2,1)}, bf16[3,256,1408]{2,1,0:T(8,128)(2,1)}, u32[]{:S(2)}, u32[]{:S(2)}) %collective-permute-start.56) | collective-permute-done | bytes 2162720 | tf_op jit(solution)/shard_map/ppermute | solution.py:178
  1423.5 16.9 collective-permute-done.58.even_ref
  1447.0 12.5 collective-permute-done.59.even_ref
  1488.1 17.7 %collective-permute-done.65.even_ref = bf16[3,256,1408]{2,1,0:T(8,128)(2,1)} collective-permute-done((bf16[3,256,1408]{2,1,0:T(8,128)(2,1)}, bf16[3,256,1408]{2,1,0:T(8,128)(2,1)}, u32[]{:S(2)}, u32[]{:S(2)}) %collective-permute-start.65) | collective-permute-done | bytes 2162720 | tf_op jit(solution)/shard_map/ppermute | solution.py:178
  1507.1 60.0 %collective-permute-done.66.even_ref = bf16[1,256,1408]{2,1,0:T(8,128)(2,1)} collective-permute-done((bf16[1,256,1408]{2,1,0:T(8,128)(2,1)S(1)}, bf16[1,256,1408]{2,1,0:T(8,128)(2,1)}, u32[]{:S(2)}, u32[]{:S(2)}) %collective-permute-start.66) | collective-permute-done | bytes 720928 | tf_op jit(solution)/shard_map/ppermute | solution.py:178
  1568.6 16.0 collective-permute-done.67.even_ref
  1618.0 31.4 %collective-permute-done.76.even_ref = bf16[3,256,1408]{2,1,0:T(8,128)(2,1)} collective-permute-done((bf16[3,256,1408]{2,1,0:T(8,128)(2,1)}, bf16[3,256,1408]{2,1,0:T(8,128)(2,1)}, u32[]{:S(2)}, u32[]{:S(2)}) %collective-permute-start.76) | collective-permute-done | bytes 2162720 | tf_op jit(solution)/shard_map/ppermute | solution.py:178
  (341 shorter events, 928.9 us)
Async XLA Ops:
  80.1 651.0 %collective-permute-start.10 = (bf16[1,256,1408]{2,1,0:T(8,128)(2,1)}, bf16[1,256,1408]{2,1,0:T(8,128)(2,1)}, u32[]{:S(2)}, u32[]{:S(2)}) collective-permute-start(bf16[1,256,1408]{2,1,0:T(8,128)(2,1)} %get-tuple-element.137), channel_id=1, source_target_pairs={{0,4},{1,5},{2,6},{3,7},{4,0},{5,1},{6,2},{7,3}} | collective-permute-start | bytes 2162696 | tf_op jit(solution)/shard_map/ppermute | solution.py:178
  81.1 652.0 %collective-permute-start.11 = (bf16[1,256,1408]{2,1,0:T(8,128)(2,1)}, bf16[1,256,1408]{2,1,0:T(8,128)(2,1)}, u32[]{:S(2)}, u32[]{:S(2)}) collective-permute-start(bf16[1,256,1408]{2,1,0:T(8,128)(2,1)} %get-tuple-element.138), channel_id=1, source_target_pairs={{0,5},{1,4},{2,7},{3,6},{4,1},{5,0},{6,3},{7,2}} | collective-permute-start | bytes 2162696 | tf_op jit(solution)/shard_map/ppermute | solution.py:178
  82.7 659.8 %collective-permute-start.12 = (bf16[1,256,1408]{2,1,0:T(8,128)(2,1)}, bf16[1,256,1408]{2,1,0:T(8,128)(2,1)}, u32[]{:S(2)}, u32[]{:S(2)}) collective-permute-start(bf16[1,256,1408]{2,1,0:T(8,128)(2,1)} %get-tuple-element.139), channel_id=1, source_target_pairs={{0,6},{1,7},{2,4},{3,5},{4,2},{5,3},{6,0},{7,1}} | collective-permute-start | bytes 2162696 | tf_op jit(solution)/shard_map/ppermute | solution.py:178
  173.9 131.9 %all-to-all-start.1 = ((bf16[16,256,1408]{2,1,0:T(8,128)(2,1)}), bf16[16,256,1408]{2,1,0:T(8,128)(2,1)}, u32[]{:S(2)}, u32[]{:S(2)}) async-start(bf16[16,256,1408]{2,1,0:T(8,128)(2,1)} %get-tuple-element.143), calls=%async_computation.1 | async-start | bytes 23068672 | tf_op jit(solution)/shard_map/all_to_all | solution.py:175
  502.1 225.4 %all-to-all-start.3 = ((bf16[8,256,1408]{2,1,0:T(8,128)(2,1)}), bf16[8,256,1408]{2,1,0:T(8,128)(2,1)}, u32[]{:S(2)}, u32[]{:S(2)}) async-start(bf16[8,256,1408]{2,1,0:T(8,128)(2,1)} %bitcast.146), calls=%async_computation.3 | async-start | bytes 11534336 | tf_op jit(solution)/shard_map/all_to_all | solution.py:175
  547.4 121.5 %collective-permute-start.16 = (bf16[4,256,1408]{2,1,0:T(8,128)(2,1)}, bf16[4,256,1408]{2,1,0:T(8,128)(2,1)}, u32[]{:S(2)}, u32[]{:S(2)}) collective-permute-start(bf16[4,256,1408]{2,1,0:T(8,128)(2,1)} %get-tuple-element.150.even_ref), channel_id=1, source_target_pairs={{0,2},{1,3},{2,0},{3,1},{4,6},{5,7},{6,4},{7,5}} | collective-permute-start | bytes 8650760 | tf_op jit(solution)/shard_map/ppermute | solution.py:178
  547.9 122.4 %collective-permute-start.17 = (bf16[4,256,1408]{2,1,0:T(8,128)(2,1)}, bf16[4,256,1408]{2,1,0:T(8,128)(2,1)}, u32[]{:S(2)}, u32[]{:S(2)}) collective-permute-start(bf16[4,256,1408]{2,1,0:T(8,128)(2,1)} %get-tuple-element.181.even_ref), channel_id=1, source_target_pairs={{0,4},{1,5},{2,6},{3,7},{4,0},{5,1},{6,2},{7,3}} | collective-permute-start | bytes 8650760 | tf_op jit(solution)/shard_map/ppermute | solution.py:178
  727.4 222.0 %all-to-all-start.4 = ((bf16[8,256,1408]{2,1,0:T(8,128)(2,1)}), bf16[8,256,1408]{2,1,0:T(8,128)(2,1)}, u32[]{:S(2)}, u32[]{:S(2)}) async-start(bf16[8,256,1408]{2,1,0:T(8,128)(2,1)} %bitcast.145), calls=%async_computation.4 | async-start | bytes 11534336 | tf_op jit(solution)/shard_map/all_to_all | solution.py:175
  731.1 80.9 %collective-permute-start.8 = (bf16[1,256,1408]{2,1,0:T(8,128)(2,1)}, bf16[1,256,1408]{2,1,0:T(8,128)(2,1)S(1)}, u32[]{:S(2)}, u32[]{:S(2)}) collective-permute-start(bf16[1,256,1408]{2,1,0:T(8,128)(2,1)} %get-tuple-element.135), channel_id=1, source_target_pairs={{0,2},{1,3},{2,0},{3,1},{4,6},{5,7},{6,4},{7,5}} | collective-permute-start | bytes 2162696 | tf_op jit(solution)/shard_map/ppermute | solution.py:178
  733.1 93.3 %collective-permute-start.9 = (bf16[1,256,1408]{2,1,0:T(8,128)(2,1)}, bf16[1,256,1408]{2,1,0:T(8,128)(2,1)S(1)}, u32[]{:S(2)}, u32[]{:S(2)}) collective-permute-start(bf16[1,256,1408]{2,1,0:T(8,128)(2,1)} %get-tuple-element.136), channel_id=1, source_target_pairs={{0,3},{1,2},{2,1},{3,0},{4,7},{5,6},{6,5},{7,4}} | collective-permute-start | bytes 2162696 | tf_op jit(solution)/shard_map/ppermute | solution.py:178
  742.5 216.4 %collective-permute-start.27 = (bf16[4,256,1408]{2,1,0:T(8,128)(2,1)}, bf16[4,256,1408]{2,1,0:T(8,128)(2,1)}, u32[]{:S(2)}, u32[]{:S(2)}) collective-permute-start(bf16[4,256,1408]{2,1,0:T(8,128)(2,1)} %get-tuple-element.181.even_ref), channel_id=1, source_target_pairs={{0,1},{1,0},{2,3},{3,2},{4,5},{5,4},{6,7},{7,6}} | collective-permute-start | bytes 8650760 | tf_op jit(solution)/shard_map/ppermute | solution.py:178
  742.7 227.1 %collective-permute-start.26 = (bf16[4,256,1408]{2,1,0:T(8,128)(2,1)}, bf16[4,256,1408]{2,1,0:T(8,128)(2,1)}, u32[]{:S(2)}, u32[]{:S(2)}) collective-permute-start(bf16[4,256,1408]{2,1,0:T(8,128)(2,1)} %get-tuple-element.150.even_ref), channel_id=1, source_target_pairs={{0,1},{1,0},{2,3},{3,2},{4,5},{5,4},{6,7},{7,6}} | collective-permute-start | bytes 8650760 | tf_op jit(solution)/shard_map/ppermute | solution.py:178
  743.0 176.9 %collective-permute-start.18 = (bf16[4,256,1408]{2,1,0:T(8,128)(2,1)}, bf16[4,256,1408]{2,1,0:T(8,128)(2,1)}, u32[]{:S(2)}, u32[]{:S(2)}) collective-permute-start(bf16[4,256,1408]{2,1,0:T(8,128)(2,1)} %collective-permute-done.14.even_ref), channel_id=1, source_target_pairs={{0,4},{1,5},{2,6},{3,7},{4,0},{5,1},{6,2},{7,3}} | collective-permute-start | bytes 8650760 | tf_op jit(solution)/shard_map/ppermute | solution.py:178
  812.0 107.9 %collective-permute-start.19 = (bf16[4,256,1408]{2,1,0:T(8,128)(2,1)S(1)}, bf16[4,256,1408]{2,1,0:T(8,128)(2,1)}, u32[]{:S(2)}, u32[]{:S(2)}) collective-permute-start(bf16[4,256,1408]{2,1,0:T(8,128)(2,1)S(1)} %copy-done.7), channel_id=1, source_target_pairs={{0,2},{1,3},{2,0},{3,1},{4,6},{5,7},{6,4},{7,5}} | collective-permute-start | bytes 8650760 | tf_op jit(solution)/shard_map/ppermute | solution.py:178
  827.2 142.6 %collective-permute-start.25 = (bf16[4,256,1408]{2,1,0:T(8,128)(2,1)}, bf16[4,256,1408]{2,1,0:T(8,128)(2,1)}, u32[]{:S(2)}, u32[]{:S(2)}) collective-permute-start(bf16[4,256,1408]{2,1,0:T(8,128)(2,1)} %collective-permute-done.14.even_ref), channel_id=1, source_target_pairs={{0,1},{1,0},{2,3},{3,2},{4,5},{5,4},{6,7},{7,6}} | collective-permute-start | bytes 8650760 | tf_op jit(solution)/shard_map/ppermute | solution.py:178
  1040.4 126.9 %all-to-all-start.5 = ((bf16[8,256,1408]{2,1,0:T(8,128)(2,1)}), bf16[8,256,1408]{2,1,0:T(8,128)(2,1)}, u32[]{:S(2)}, u32[]{:S(2)}) async-start(bf16[8,256,1408]{2,1,0:T(8,128)(2,1)} %bitcast.144), calls=%async_computation.5 | async-start | bytes 11534336 | tf_op jit(solution)/shard_map/all_to_all | solution.py:175
  1044.0 78.1 %collective-permute-start.37 = (bf16[4,256,1408]{2,1,0:T(8,128)(2,1)}, bf16[4,256,1408]{2,1,0:T(8,128)(2,1)}, u32[]{:S(2)}, u32[]{:S(2)}) collective-permute-start(bf16[4,256,1408]{2,1,0:T(8,128)(2,1)} %collective-permute-done.29.even_ref), channel_id=1, source_target_pairs={{0,1},{1,0},{2,3},{3,2},{4,5},{5,4},{6,7},{7,6}} | collective-permute-start | bytes 8650760 | tf_op jit(solution)/shard_map/ppermute | solution.py:178
  1106.1 121.2 %collective-permute-start.40 = (bf16[4,256,1408]{2,1,0:T(8,128)(2,1)}, bf16[4,256,1408]{2,1,0:T(8,128)(2,1)}, u32[]{:S(2)}, u32[]{:S(2)}) collective-permute-start(bf16[4,256,1408]{2,1,0:T(8,128)(2,1)} %get-tuple-element.198.even_ref), channel_id=1, source_target_pairs={{0,2},{1,3},{2,0},{3,1},{4,6},{5,7},{6,4},{7,5}} | collective-permute-start | bytes 8650760 | tf_op jit(solution)/shard_map/ppermute | solution.py:178
  1122.1 106.3 %collective-permute-start.41 = (bf16[4,256,1408]{2,1,0:T(8,128)(2,1)}, bf16[4,256,1408]{2,1,0:T(8,128)(2,1)}, u32[]{:S(2)}, u32[]{:S(2)}) collective-permute-start(bf16[4,256,1408]{2,1,0:T(8,128)(2,1)} %get-tuple-element.200.even_ref), channel_id=1, source_target_pairs={{0,4},{1,5},{2,6},{3,7},{4,0},{5,1},{6,2},{7,3}} | collective-permute-start | bytes 8650760 | tf_op jit(solution)/shard_map/ppermute | solution.py:178
  1127.7 101.6 %collective-permute-start.43 = (bf16[4,256,1408]{2,1,0:T(8,128)(2,1)}, bf16[4,256,1408]{2,1,0:T(8,128)(2,1)}, u32[]{:S(2)}, u32[]{:S(2)}) collective-permute-start(bf16[4,256,1408]{2,1,0:T(8,128)(2,1)} %get-tuple-element.200.even_ref), channel_id=1, source_target_pairs={{0,1},{1,0},{2,3},{3,2},{4,5},{5,4},{6,7},{7,6}} | collective-permute-start | bytes 8650760 | tf_op jit(solution)/shard_map/ppermute | solution.py:178
  1486.2 98.4 %collective-permute-start.71 = (bf16[3,256,1408]{2,1,0:T(8,128)(2,1)}, bf16[3,256,1408]{2,1,0:T(8,128)(2,1)}, u32[]{:S(2)}, u32[]{:S(2)}) collective-permute-start(bf16[3,256,1408]{2,1,0:T(8,128)(2,1)} %collective-permute-done.64.even_ref), channel_id=1, source_target_pairs={{0,1},{1,0},{2,3},{3,2},{4,5},{5,4},{6,7},{7,6}} | collective-permute-start | bytes 6488072 | tf_op jit(solution)/shard_map/ppermute | solution.py:178
  1486.2 113.3 %collective-permute-start.72 = (bf16[4,256,1408]{2,1,0:T(8,128)(2,1)}, bf16[4,256,1408]{2,1,0:T(8,128)(2,1)}, u32[]{:S(2)}, u32[]{:S(2)}) collective-permute-start(bf16[4,256,1408]{2,1,0:T(8,128)(2,1)} %collective-permute-done.40.even_ref), channel_id=1, source_target_pairs={{0,4},{1,5},{2,6},{3,7},{4,0},{5,1},{6,2},{7,3}} | collective-permute-start | bytes 8650760 | tf_op jit(solution)/shard_map/ppermute | solution.py:178
  1486.8 112.8 %collective-permute-start.73 = (bf16[4,256,1408]{2,1,0:T(8,128)(2,1)}, bf16[4,256,1408]{2,1,0:T(8,128)(2,1)}, u32[]{:S(2)}, u32[]{:S(2)}) collective-permute-start(bf16[4,256,1408]{2,1,0:T(8,128)(2,1)} %collective-permute-done.41.even_ref), channel_id=1, source_target_pairs={{0,2},{1,3},{2,0},{3,1},{4,6},{5,7},{6,4},{7,5}} | collective-permute-start | bytes 8650760 | tf_op jit(solution)/shard_map/ppermute | solution.py:178
  1505.8 84.0 %collective-permute-start.70 = (bf16[3,256,1408]{2,1,0:T(8,128)(2,1)}, bf16[3,256,1408]{2,1,0:T(8,128)(2,1)}, u32[]{:S(2)}, u32[]{:S(2)}) collective-permute-start(bf16[3,256,1408]{2,1,0:T(8,128)(2,1)} %collective-permute-done.65.even_ref), channel_id=1, source_target_pairs={{0,1},{1,0},{2,3},{3,2},{4,5},{5,4},{6,7},{7,6}} | collective-permute-start | bytes 6488072 | tf_op jit(solution)/shard_map/ppermute | solution.py:178
  (97 other events, 3017.5 us)
